TPU v7x, 512 devices: a 8x2x16 block of a 8x16x16 slice. The times are simulated.
512 devices in a mesh: chan: 2 (over y), row: 128 (over z, x), col: 2 (over core).
Axes of the slice: x: 8, y: 2, z: 16, core: 2. Of those that a mesh axis runs over, the one named last changes fastest.
The devices are a block of a 8x16x16 slice.
Arguments:
- hamiltonian_rows: float32 [256, 2, 2, 65536], P('chan', 'col', None, 'row'), parts along dimension 0, may hold values from -2 to 2, as said below
- current_block: float32 [131072, 256], P(('chan', 'row', 'col')), parts along dimension 0, may hold values from -6 to 6
- correction_block: float32 [131072, 256], P(('chan', 'row', 'col')), parts along dimension 0, may hold values from -6 to 6
- previous_block: float32 [131072, 256], P(('chan', 'row', 'col')), parts along dimension 0, may hold values from -6 to 6
- ritz_values: float32 [512], P('chan'), parts along dimension 0, may hold values from -2 to 2
- mixing_coeffs: float32 [1536, 256], P('chan'), parts along dimension 0, may hold values from -0.21875 to 0.21875
Outputs:
- next_block: float32 [1024, 256], P(('chan', 'row', 'col')), parts along dimension 0
- next_direction: float32 [1024, 256], P(('chan', 'row', 'col')), parts along dimension 0
- next_correction: float32 [1024, 256], P(('chan', 'row', 'col')), parts along dimension 0
- ritz_matrix: float32 [512, 256], P('chan'), parts along dimension 0
- metric_matrix: float32 [512, 256], P('chan'), parts along dimension 0
There are 2 independent parts, one for each index of `chan`. A program takes and returns all parts, laid end to end along the dimension named above; each array names one. Nothing has to cross between parts.
Inputs may be any that keep to these rules, and one draw needn't show every extreme that they name: hamiltonian_rows[a, b, j, :] is row (a * 2 + b) * 256 + j of the channel's Hamiltonian; its entry in that row's own column is the onsite energy.
All inputs are finite; a program needn't handle non-finite values.
Results may differ from a plain program's by a relative error of at most 0.00008.
Values sent between devices are 32-bit elements; how exact they have to be, the bound alone decides.
A program may use at most 64 MiB of HBM per device.

v0:
```python
import jax
import jax.numpy as jnp
from jax import lax
from jax.sharding import Mesh
from jax.sharding import PartitionSpec as P

ROW = ("row_0", "row_1")
ROW_COL = ("row_0", "row_1", "col")
CHAN_ROW_COL = ("chan", "row_0", "row_1", "col")


def copy_for_each(shard, axis):
    count = lax.axis_size(axis)
    return lax.all_to_all(
        jnp.broadcast_to(shard[None], (count, *shard.shape)), axis, 0, 0, tiled=True
    )


def laid_out(blocks, dim):
    lengths = list(blocks.shape[1:])
    lengths[dim] *= blocks.shape[0]
    return jnp.moveaxis(blocks, 0, dim).reshape(lengths)


def gather_directly(shard, axis, dim):
    blocks = copy_for_each(shard, axis)
    return laid_out(blocks, dim)


def sum_by_axis(running, axes):
    for axis in axes:
        running = lax.psum_scatter(running, axis, scatter_dimension=0, tiled=True)
    return running


def packed_total(arrays, axis):
    ends = [0]
    for a in arrays:
        ends.append(ends[-1] + a.size)
    running = lax.psum(jnp.concatenate([a.ravel() for a in arrays]), axis)
    return tuple((running[b:e].reshape(a.shape) for a, b, e in zip(arrays, ends, ends[1:])))


def matmul(left, right):
    return jnp.dot(left, right, preferred_element_type=jnp.float32, precision=lax.Precision.HIGHEST)


def tmatmul(left, right):
    return lax.dot_general(
        left,
        right,
        (((0,), (0,)), ((), ())),
        preferred_element_type=jnp.float32,
        precision=lax.Precision.HIGHEST,
    )


def upper_blocks(gram_matrix, block_width):
    pieces = []
    for left_index in range(3):
        for right_index in range(left_index, 3):
            pieces.append(
                gram_matrix[
                    left_index * block_width : (left_index + 1) * block_width,
                    right_index * block_width : (right_index + 1) * block_width,
                ]
            )
    return jnp.stack(pieces)


def full_gram(stacked):
    lookup = {(0, 0): 0, (0, 1): 1, (0, 2): 2, (1, 1): 3, (1, 2): 4, (2, 2): 5}
    row_parts = []
    for left_index in range(3):
        column_parts = []
        for right_index in range(3):
            if left_index <= right_index:
                column_parts.append(stacked[lookup[left_index, right_index]])
            else:
                column_parts.append(stacked[lookup[right_index, left_index]].T)
        row_parts.append(jnp.concatenate(column_parts, axis=1))
    return jnp.concatenate(row_parts, axis=0)


def on_device(
    hamiltonian_rows, current_block, correction_block, previous_block, ritz_values, mixing_coeffs
):
    block_width = current_block.shape[1]
    out_rows = hamiltonian_rows.shape[2]
    window_total = out_rows * lax.axis_size(ROW) * lax.axis_size("col")
    own_rows = jnp.concatenate([current_block, correction_block, previous_block], axis=1)
    window_rows = own_rows[:out_rows]
    basis_part = upper_blocks(tmatmul(window_rows, window_rows), block_width)
    gathered = gather_directly(own_rows, "col", 0)
    local_tile = hamiltonian_rows.reshape(-1, hamiltonian_rows.shape[3])
    product_rows = sum_by_axis(matmul(local_tile, gathered), ROW)
    residual = product_rows[:, :block_width] - window_rows[:, :block_width] * ritz_values[None, :]
    squares = jnp.sum(residual * residual, axis=0)
    product_part = tmatmul(window_rows, product_rows)
    basis_sum, product_sum, square_sum = packed_total((basis_part, product_part, squares), ROW_COL)
    next_block = matmul(window_rows, mixing_coeffs)
    metric_gram = full_gram(basis_sum)
    ritz_matrix = tmatmul(mixing_coeffs, matmul(product_sum, mixing_coeffs))
    metric_matrix = tmatmul(mixing_coeffs, matmul(metric_gram, mixing_coeffs))
    next_direction = matmul(window_rows[:, block_width:], mixing_coeffs[block_width:, :])
    next_correction = residual * lax.rsqrt(square_sum / window_total + 1e-06)
    return (next_block, next_direction, next_correction, ritz_matrix, metric_matrix)


def solution(mesh):
    finer = Mesh(
        mesh.devices.reshape(mesh.shape["chan"], 16, 8, mesh.shape["col"]),
        ("chan", "row_0", "row_1", "col"),
    )
    in_specs = (
        P("chan", "col", None, ROW),
        P(CHAN_ROW_COL, None),
        P(CHAN_ROW_COL, None),
        P(CHAN_ROW_COL, None),
        P("chan"),
        P("chan", None),
    )
    out_specs = (
        P(CHAN_ROW_COL, None),
        P(CHAN_ROW_COL, None),
        P(CHAN_ROW_COL, None),
        P("chan", None),
        P("chan", None),
    )
    return jax.shard_map(
        on_device, mesh=finer, in_specs=in_specs, out_specs=out_specs, check_vma=False
    )
```

profile of v0, /device:TPU:65, one launch (start us, length us, event | category | flops | bytes accessed | tf_op | source)
XLA Modules:
  0.0 563.5 jit_solution(1602862439774385199)
XLA Ops:
  7.2 1.0 constant_dynamic-update-slice_fusion.2
  8.2 1.0 constant_dynamic-update-slice_fusion.1
  9.1 1.0 constant_dynamic-update-slice_fusion
  10.1 0.9 copy-done.1
  11.0 1.3 broadcast_in_dim.2
  12.3 45.1 %all-to-all-start = ((f32[2,256,768]{2,1,0:T(8,128)}), f32[2,256,768]{2,1,0:T(8,128)S(1)}, u32[]{:S(2)}, u32[]{:S(2)}) async-start(f32[2,256,768]{2,1,0:T(8,128)} %broadcast_in_dim.2), calls=%async_computation | async-start | bytes 3145728 | tf_op jit(solution)/shard_map/all_to_all | solution.py:14
  57.7 1.8 all-to-all-done
  59.5 2.6 convolution_bitcast_fusion
  62.1 1.2 copy.51
  63.4 2.9 fusion.26
  66.5 2.0 copy.56
  68.5 1.3 dynamic-slice
  70.4 49.3 %reduce-scatter.5.cloned.1.call-done = f32[16,768]{1,0:T(8,128)} async-done(((f32[256,768]{1,0:T(8,128)}), f32[16,768]{1,0:T(8,128)}) %reduce-scatter.5.cloned.1.call-update) | async-done | bytes 49168
  119.7 1.0 copy.52
  120.7 27.3 %all-reduce = f32[16,768]{0,1:T(8,128)S(1)} all-reduce(f32[16,768]{0,1:T(8,128)S(1)} %copy.52), channel_id=3, replica_groups=mesh['chan'=2,'row_0'=16,'row_1'=8,'col'=2] {'row_1'}, use_global_device_ids=true, to_apply=%region_1.0.clone | all-reduce | flops 12288 | bytes 98304
  148.0 2.9 fusion.16
  151.1 1.6 reshape.98
  153.3 4.3 pad_maximum_fusion
  157.7 1.1 copy-done
  158.9 0.9 fusion.14
  159.8 1.7 fusion.28
  161.5 371.7 %all-reduce.3.cloned.1.call-done = f32[983296]{0:T(1024)} async-done(((f32[983296]{0:T(1024)}), f32[983296]{0:T(1024)}) %all-reduce.3.cloned.1.call-update) | async-done | bytes 3933200 | tf_op jit(solution)/shard_map/psum | solution.py:40
  533.9 1.3 broadcast_multiply_fusion
  535.2 3.3 slice.176
  538.4 2.7 reshape.99
  541.1 2.0 fusion.36
  543.1 1.5 convolution_bitcast_fusion.2
  544.6 0.8 copy.49
  545.4 1.4 fusion.35
  547.4 0.8 copy.47
  549.5 4.9 fusion
  554.4 1.5 convolution_bitcast_fusion.1
  (36 shorter events, 4.9 us)
Async XLA Ops:
  10.1 0.9 copy-start.1
  11.0 46.4 %copy-start.4 = (f32[128,1,2,512]{3,2,1,0:T(2,128)S(1)}, f32[128,1,2,512]{3,2,1,0:T(2,128)}, u32[]{:S(2)}) copy-start(f32[128,1,2,512]{3,2,1,0:T(2,128)} %param.6) | copy-start | bytes 1572868
  12.3 47.2 %all-to-all-start = ((f32[2,256,768]{2,1,0:T(8,128)}), f32[2,256,768]{2,1,0:T(8,128)S(1)}, u32[]{:S(2)}, u32[]{:S(2)}) async-start(f32[2,256,768]{2,1,0:T(8,128)} %broadcast_in_dim.2), calls=%async_computation | async-start | bytes 3145728 | tf_op jit(solution)/shard_map/all_to_all | solution.py:14
  57.4 62.3 %reduce-scatter.5.cloned.1.call-start = ((), (), s32[]{:S(2)}) async-start(), calls=%async_computation.3 | async-start | bytes 835584
  63.3 469.9 %all-reduce.3.cloned.1.call-start = ((), (), s32[]{:S(2)}) async-start(), calls=%async_computation.2 | async-start | bytes 7872512 | tf_op jit(solution)/shard_map/psum | solution.py:40
  151.1 1.6 copy-start.5
  157.6 1.1 copy-start
  157.6 1.2 copy-start.2
  157.6 1.3 copy-start.3
Sparse Core Ops, SparseCore 0:
  63.5 56.1 reduce-scatter.4
  157.8 375.3 all-reduce.2
where the time goes:
time: 564 us
  waiting for transfers between devices  423 us (75%)
  starting transfers between devices  45.2 us (8%)
  blocking collectives  27.3 us (5%)
  local copies, waits for them, and re-layouts  25.4 us (5%)
  matrix products  20.9 us (4%)
  between operations  14.9 us (3%)
  other arithmetic  7.02 us (1%)
    psum x1, waiting for transfers between devices, packed_total(): running = lax.psum(jnp.concatenate([a.ravel() for a in arrays]), axis)  372 us
    unnamed x3, waiting for transfers between devices  49.4 us
    all_to_all x1, starting transfers between devices, copy_for_each(): lax.all_to_all(jnp.broadcast_to(shard[None], (count, *shard.shape)), axis...  45.1 us
    unnamed x1, blocking collectives  27.3 us
    dot_general x5, matrix products, matmul(): jnp.dot(left, right, preferred_element_type=jnp.float32, precision=lax.Pr...  12.1 us
  transfers between devices with their start and end apart: 3, of which 3 were waited for; matrix products, arithmetic and copies ran while one was open for 2% of the time, Pallas kernels for 0%

commit v1 on v0

v1 whole, which is shorter than its diff:
```python
import functools

import jax
import jax.numpy as jnp
from jax import lax
from jax.experimental import pallas as pl
from jax.experimental.pallas import tpu as pltpu
from jax.sharding import Mesh
from jax.sharding import PartitionSpec as P

NZ, NX = 16, 8
ROW = ("row_0", "row_1")
CHAN_ROW_COL = ("chan", "row_0", "row_1", "col")
MESH = pl.DeviceIdType.MESH
LANES = 128
HIGHEST = lax.Precision.HIGHEST


def dot(left, right):
    return jnp.dot(left, right, preferred_element_type=jnp.float32, precision=HIGHEST)


def tdot(left, right):
    return lax.dot_general(
        left,
        right,
        (((0,), (0,)), ((), ())),
        preferred_element_type=jnp.float32,
        precision=HIGHEST,
    )


def kernel(
    nz,
    nx,
    window_total,
    h_ref,
    x_ref,
    w_ref,
    p_ref,
    c_ref,
    rv_ref,
    nb_ref,
    nd_ref,
    nc_ref,
    ritz_ref,
    metric_ref,
    y_own,
    x_par,
    y_par,
    part,
    in_x,
    mid,
    in_z,
    tile,
    all_z,
    pack,
    all_x,
    nb_tile,
    nb_all_z,
    nb_pack,
    nb_all_x,
    core_own,
    core_par,
    sq_own,
    sq_par,
    xs_sem,
    xr_sem,
    zs_sem,
    zr_sem,
    azs_sem,
    azr_sem,
    axs_sem,
    axr_sem,
    nzs_sem,
    nzr_sem,
    nxs_sem,
    nxr_sem,
    cs_sem,
    cr_sem,
):
    z = lax.axis_index("row_0")
    x = lax.axis_index("row_1")
    core = lax.axis_index("col")
    other = 1 - core
    owners = nz * nx
    half = x_ref.shape[0]
    far_z = sorted(range(1, nz), key=lambda d: -min(d, nz - d))
    far_x = sorted(range(1, nx), key=lambda d: -min(d, nx - d))

    def plus_z(d):
        return lax.rem(z + d, nz)

    def plus_x(d):
        return lax.rem(x + d, nx)

    def remote(src, dst, send, recv, device):
        return pltpu.make_async_remote_copy(
            src_ref=src, dst_ref=dst, send_sem=send, recv_sem=recv, device_id=device, device_id_type=MESH
        )

    def send_z(src, dst, d, send, recv):
        copy = remote(src, dst.at[z], send.at[d], recv.at[z], {"row_0": plus_z(d)})
        copy.start()
        return copy

    def got_z(src, dst, d, send, recv):
        s = plus_z(d)
        remote(src, dst.at[s], send.at[d], recv.at[s], {"row_0": s}).wait_recv()

    def send_x(src, dst, d, send, recv):
        copy = remote(src, dst.at[x], send.at[d], recv.at[x], {"row_1": plus_x(d)})
        copy.start()
        return copy

    def got_x(src, dst, d, send, recv):
        s = plus_x(d)
        remote(src, dst.at[s], send.at[d], recv.at[s], {"row_1": s}).wait_recv()

    def core_copy(src, dst, i):
        copy = remote(src, dst, cs_sem.at[i], cr_sem.at[i], {"col": other})
        copy.start()
        return copy

    barrier = pltpu.get_barrier_semaphore()
    for d in range(1, nz):
        pl.semaphore_signal(barrier, inc=1, device_id={"row_0": plus_z(d)}, device_id_type=MESH)
    for d in range(1, nx):
        pl.semaphore_signal(barrier, inc=1, device_id={"row_1": plus_x(d)}, device_id_type=MESH)
    pl.semaphore_signal(barrier, inc=1, device_id={"col": other}, device_id_type=MESH)

    direction = dot(w_ref[...], c_ref[half : 2 * half, :]) + dot(p_ref[...], c_ref[2 * half :, :])
    nd_ref[...] = direction[:2, :]
    y_own[...] = direction + dot(x_ref[...], c_ref[:half, :])
    nb_ref[...] = y_own[0:2, :]
    nb_tile[...] = jnp.zeros_like(nb_tile)
    for j in range(2):
        for q in range(2):
            nb_tile[j * 4 + q : j * 4 + q + 1, :] = y_own[j : j + 1, q * LANES : (q + 1) * LANES]

    pl.semaphore_wait(barrier, nz + nx - 1)

    copies = []
    x_core = core_copy(x_ref, x_par, 0)
    y_core = core_copy(y_own, y_par, 1)
    for d in far_z:
        copies.append(send_z(nb_tile, nb_all_z, d, nzs_sem, nzr_sem))

    def h_cols(which):
        tiles = half // LANES
        rows = []
        for j in range(2):
            rows.append(
                jnp.concatenate(
                    [h_ref[pl.ds((which * tiles + t) * 2 + j, owners, stride=8), :] for t in range(tiles)], axis=1
                )
            )
        return jnp.concatenate(rows, axis=0)

    def put(value, first):
        for j in range(2):
            for q in range(2):
                block = value[j * owners : (j + 1) * owners, q * LANES : (q + 1) * LANES]
                part[:, :, j * 4 + first + q, :] = block.reshape(nz, nx, LANES)

    h_own = h_cols(core)
    h_par = h_cols(other)
    hx = dot(h_own, x_ref[...])
    hy = dot(h_own, y_own[...])
    x_core.wait_recv()
    put(hx + dot(h_par, x_par[...]), 0)
    y_core.wait_recv()
    put(hy + dot(h_par, y_par[...]), 2)

    for d in far_x:
        copies.append(send_x(part.at[:, plus_x(d)], in_x, d, xs_sem, xr_sem))

    def repack(source, first, packed):
        for j in range(2):
            for q in range(2):
                packed[(j * 2 + q) * nz : (j * 2 + q + 1) * nz, :] = source[:, j * 4 + first + q, :]

    nb_all_z[z] = nb_tile[...]
    for d in range(1, nz):
        got_z(nb_tile, nb_all_z, d, nzs_sem, nzr_sem)
    repack(nb_all_z, 0, nb_pack)
    nb_all_x[x] = nb_pack[...]
    for d in far_x:
        copies.append(send_x(nb_pack, nb_all_x, d, nxs_sem, nxr_sem))

    for d in range(1, nx):
        got_x(part.at[:, x], in_x, d, xs_sem, xr_sem)
    total = part[:, x]
    for d in range(1, nx):
        total = total + in_x[plus_x(d)]
    mid[...] = total

    for d in far_z:
        copies.append(send_z(mid.at[plus_z(d)], in_z, d, zs_sem, zr_sem))
    own_sum = mid[z]
    for d in range(1, nz):
        got_z(mid.at[z], in_z, d, zs_sem, zr_sem)
    for d in range(1, nz):
        own_sum = own_sum + in_z[plus_z(d)]
    tile[...] = own_sum

    residual = []
    for j in range(2):
        residual.append(
            [
                tile[j * 4 + q : j * 4 + q + 1, :]
                - x_ref[j : j + 1, q * LANES : (q + 1) * LANES] * rv_ref[:, q * LANES : (q + 1) * LANES]
                for q in range(2)
            ]
        )
    for q in range(2):
        tile[q : q + 1, :] = residual[0][q] * residual[0][q] + residual[1][q] * residual[1][q]

    for d in far_z:
        copies.append(send_z(tile, all_z, d, azs_sem, azr_sem))
    all_z[z] = tile[...]
    for d in range(1, nz):
        got_z(tile, all_z, d, azs_sem, azr_sem)
    repack(all_z, 2, pack)
    pack[4 * nz :, :] = jnp.zeros((8, LANES), jnp.float32)
    for q in range(2):
        pack[4 * nz + q : 4 * nz + q + 1, :] = jnp.sum(all_z[:, q, :], axis=0, keepdims=True)
    for d in far_x:
        copies.append(send_x(pack, all_x, d, axs_sem, axr_sem))
    all_x[x] = pack[...]

    def rows_of(source):
        columns = []
        for q in range(2):
            columns.append(
                jnp.concatenate(
                    [source[:, (j * 2 + q) * nz : (j * 2 + q + 1) * nz, :].reshape(owners, LANES) for j in range(2)],
                    axis=0,
                )
            )
        return jnp.concatenate(columns, axis=1)

    for d in range(1, nx):
        got_x(nb_pack, nb_all_x, d, nxs_sem, nxr_sem)
    nb_rows = rows_of(nb_all_x)
    core_own[0] = tdot(nb_rows, nb_rows)
    metric_core = core_copy(core_own.at[0], core_par.at[0], 2)

    for d in range(1, nx):
        got_x(pack, all_x, d, axs_sem, axr_sem)
    sq_own[...] = jnp.sum(all_x[:, 4 * nz :, :], axis=0)
    sq_core = core_copy(sq_own, sq_par, 3)
    core_own[1] = tdot(nb_rows, rows_of(all_x))
    ritz_core = core_copy(core_own.at[1], core_par.at[1], 4)

    metric_core.wait_recv()
    metric_ref[...] = core_own[0] + core_par[0]
    sq_core.wait_recv()
    squares = sq_own[...] + sq_par[...]
    for q in range(2):
        scale = lax.rsqrt(squares[q : q + 1, :] / window_total + 1e-06)
        for j in range(2):
            nc_ref[j : j + 1, q * LANES : (q + 1) * LANES] = residual[j][q] * scale
    ritz_core.wait_recv()
    ritz_ref[...] = core_own[1] + core_par[1]

    for copy in copies + [x_core, y_core, metric_core, sq_core, ritz_core]:
        copy.wait_send()


def on_device(hamiltonian_rows, current_block, correction_block, previous_block, ritz_values, mixing_coeffs):
    nz, nx = lax.axis_size("row_0"), lax.axis_size("row_1")
    owners, _, out_rows, columns = hamiltonian_rows.shape
    block_width = current_block.shape[1]
    window_total = out_rows * owners * lax.axis_size("col")
    tiles = columns // LANES
    h_flat = hamiltonian_rows.reshape(owners, out_rows, tiles, LANES).transpose(0, 2, 1, 3)
    h_flat = h_flat.reshape(owners * tiles * out_rows, LANES)
    f32 = functools.partial(jax.ShapeDtypeStruct, dtype=jnp.float32)
    vmem = pl.BlockSpec(memory_space=pltpu.VMEM)
    square = (block_width, block_width)

    def buffer(*shape):
        return pltpu.VMEM(shape, jnp.float32)

    sems = pltpu.SemaphoreType.DMA
    sem_sizes = (nx, nx, nz, nz, nz, nz, nx, nx, nz, nz, nx, nx, 5, 5)
    return pl.pallas_call(
        functools.partial(kernel, nz, nx, window_total),
        out_shape=(
            f32((out_rows, block_width)),
            f32((out_rows, block_width)),
            f32((out_rows, block_width)),
            f32(square),
            f32(square),
        ),
        in_specs=[vmem] * 6,
        out_specs=(vmem,) * 5,
        scratch_shapes=[
            buffer(*square),
            buffer(*square),
            buffer(*square),
            buffer(nz, nx, 8, LANES),
            buffer(nx, nz, 8, LANES),
            buffer(nz, 8, LANES),
            buffer(nz, 8, LANES),
            buffer(8, LANES),
            buffer(nz, 8, LANES),
            buffer(4 * nz + 8, LANES),
            buffer(nx, 4 * nz + 8, LANES),
            buffer(8, LANES),
            buffer(nz, 8, LANES),
            buffer(4 * nz, LANES),
            buffer(nx, 4 * nz, LANES),
            buffer(2, *square),
            buffer(2, *square),
            buffer(8, LANES),
            buffer(8, LANES),
        ]
        + [sems((n,)) for n in sem_sizes],
        compiler_params=pltpu.CompilerParams(collective_id=0, has_side_effects=True),
        name="lobpcg_step",
    )(h_flat, current_block, correction_block, previous_block, mixing_coeffs, ritz_values.reshape(1, -1))


def solution(mesh):
    finer = Mesh(
        mesh.devices.reshape(mesh.shape["chan"], NZ, NX, mesh.shape["col"]),
        ("chan", "row_0", "row_1", "col"),
    )
    in_specs = (
        P("chan", "col", None, ROW),
        P(CHAN_ROW_COL, None),
        P(CHAN_ROW_COL, None),
        P(CHAN_ROW_COL, None),
        P("chan"),
        P("chan", None),
    )
    out_specs = (
        P(CHAN_ROW_COL, None),
        P(CHAN_ROW_COL, None),
        P(CHAN_ROW_COL, None),
        P("chan", None),
        P("chan", None),
    )
    return jax.shard_map(on_device, mesh=finer, in_specs=in_specs, out_specs=out_specs, check_vma=False)
```

time: 564 us -> 101 us (0.18)
  waiting for transfers between devices: 423 us -> 0 us
  Pallas kernels: 0 us -> 94.7 us
  starting transfers between devices: 45.2 us -> 0 us
  blocking collectives: 27.3 us -> 0 us
  matrix products: 20.9 us -> 0 us
  local copies, waits for them, and re-layouts: 25.4 us -> 5 us
  between operations: 14.9 us -> 0.65 us
  other arithmetic: 7.02 us -> 0 us
    psum x1 -> x0, waiting for transfers between devices: 372 us -> none  [packed_total(): running = lax.psum(jnp.concatenate([a.ravel() for a in arrays]), axis)]
    pallas_call x0 -> x1, Pallas kernels: none -> 94.7 us  [on_device(): pl.pallas_call(functools.partial(kernel, nz, nx, window_total), out_shape...]
    unnamed x3 -> x0, waiting for transfers between devices: 49.4 us -> none
    all_to_all x1 -> x0, starting transfers between devices: 45.1 us -> none  [copy_for_each(): lax.all_to_all(jnp.broadcast_to(shard[None], (count, *shard.shape)), axis...]
    unnamed x1 -> x0, blocking collectives: 27.3 us -> none
    dot_general x9 -> x0, matrix products: 20.9 us -> none  [the longest x5 12.1 us: matmul(): jnp.dot(left, right, preferred_element_type=jnp.float32, precision=lax.Pr...]
    slice x12 -> x0, local copies, waits for them, and re-layouts: 7.03 us -> none  [the longest x10 3.69 us: full_gram(): column_parts.append(stacked[lookup[left_index, right_index]])]
    unnamed x26 -> x13, local copies, waits for them, and re-layouts: 11.2 us -> 5 us
  transfers between devices with their start and end apart: 3 -> 0, of which waited for: 3 -> 0; matrix products, arithmetic and copies ran while one was open for 2% -> 0% of each run, Pallas kernels for 0% -> 0%
where the time goes in v1:
time: 101 us; the launch traced here: 100 us
  Pallas kernels  94.7 us (94%)
  local copies, waits for them, and re-layouts  5 us (5%)
    pallas_call x1, Pallas kernels, on_device(): pl.pallas_call(functools.partial(kernel, nz, nx, window_total), out_shape...  94.7 us
    unnamed x13, local copies, waits for them, and re-layouts  5 us

profile of v1, /device:TPU:65, one launch (start us, length us, event | category | flops | bytes accessed | tf_op | source)
XLA Modules:
  0.0 100.4 jit_solution(13186859887944642822)
XLA Ops:
  0.6 94.7 %lobpcg_step.1 = (f32[2,256]{1,0:T(2,128)}, f32[2,256]{1,0:T(2,128)}, f32[2,256]{1,0:T(2,128)}, f32[256,256]{1,0:T(8,128)}, f32[256,256]{1,0:T(8,128)}) custom-call(f32[1024,128]{1,0:T(8,128)} %bitcast.6, f32[256,256]{1,0:T(8,128)} %x_ref.1, f32[256,256]{1,0:T(8,128)} %w_ref.1, f32[256,256]{1,0:T(8,128)} %p_ref.1, f32[768,256]{1,0:T(8,128)} %c_ref.1, ...), custom_call_target="tpu_custom_call" | custom-call | tf_op jit(solution)/shard_map/lobpcg_step/pallas_call | solution.py:288
  95.4 0.0 copy-start.3
  95.4 0.7 copy-done.3
  96.0 0.0 copy-start.2
  96.0 0.6 copy.17
  96.6 0.1 copy-done.2
  96.7 0.0 copy-start.1
  96.7 0.6 copy.18
  97.3 0.1 copy-done.1
  97.4 0.6 copy.19
  98.0 0.0 copy-start
  98.0 1.7 %copy.20 = f32[256,256]{1,0:T(8,128)} copy(f32[256,256]{1,0:T(8,128)} %get-tuple-element.13) | data formatting | bytes 524288
  99.7 0.0 copy-done
  99.7 0.7 copy.21
Async XLA Ops:
  95.4 0.7 copy-start.3
  96.0 0.7 copy-start.2
  96.7 0.7 copy-start.1
  98.0 1.7 %copy-start = (f32[256,256]{1,0:T(8,128)S(1)}, f32[256,256]{1,0:T(8,128)}, u32[]{:S(2)}) copy-start(f32[256,256]{1,0:T(8,128)} %get-tuple-element.14) | copy-start | bytes 786436

commit v2 on v1

v2 whole, which is shorter than its diff:
```python
import functools

import jax
import jax.numpy as jnp
from jax import lax
from jax.experimental import pallas as pl
from jax.experimental.pallas import tpu as pltpu
from jax.sharding import Mesh
from jax.sharding import PartitionSpec as P

NZ, NX = 16, 8
ROW = ("row_0", "row_1")
CHAN_ROW_COL = ("chan", "row_0", "row_1", "col")
MESH = pl.DeviceIdType.MESH
LANES = 128
MAIN_VMEM = 24 * 2**20
END_VMEM = 8 * 2**20
HIGHEST = lax.Precision.HIGHEST


def dot(left, right):
    return jnp.dot(left, right, preferred_element_type=jnp.float32, precision=HIGHEST)


def tdot(left, right):
    return lax.dot_general(
        left,
        right,
        (((0,), (0,)), ((), ())),
        preferred_element_type=jnp.float32,
        precision=HIGHEST,
    )


def kernel(
    nz,
    nx,
    h_hbm,
    x_hbm,
    w_hbm,
    p_hbm,
    c_hbm,
    rv_hbm,
    small_ref,
    ritz_ref,
    metric_ref,
    rv_ref,
    h_ref,
    x_ref,
    w_ref,
    p_ref,
    c_ref,
    y_own,
    x_par,
    y_par,
    part,
    in_x,
    mid,
    in_z,
    tile,
    all_z,
    pack,
    all_x,
    sq_tile,
    sq_all,
    nb_tile,
    nb_all_z,
    nb_pack,
    nb_all_x,
    core_own,
    core_par,
    sq_own,
    sq_par,
    in_sem,
    xs_sem,
    xr_sem,
    zs_sem,
    zr_sem,
    azs_sem,
    azr_sem,
    axs_sem,
    axr_sem,
    qs_sem,
    qr_sem,
    nzs_sem,
    nzr_sem,
    nxs_sem,
    nxr_sem,
    cs_sem,
    cr_sem,
):
    z = lax.axis_index("row_0")
    x = lax.axis_index("row_1")
    core = lax.axis_index("col")
    other = 1 - core
    owners = nz * nx
    pairs = nz // 2
    half = x_ref.shape[0]
    own_pair = z // 2
    z_mate = 2 * own_pair + 1 - lax.rem(z, 2)
    far_z = sorted(range(1, nz), key=lambda d: -min(d, nz - d))
    far_x = sorted(range(1, nx), key=lambda d: -min(d, nx - d))
    far_pairs = sorted(range(pairs), key=lambda k: -min(k, pairs - k))
    near_pairs = far_pairs[::-1]

    def plus_z(d):
        return lax.rem(z + d, nz)

    def plus_x(d):
        return lax.rem(x + d, nx)

    def pair_at(k):
        return lax.rem(own_pair + k, pairs)

    def remote(src, dst, send, recv, device):
        return pltpu.make_async_remote_copy(
            src_ref=src, dst_ref=dst, send_sem=send, recv_sem=recv, device_id=device, device_id_type=MESH
        )

    copies = []

    def send(src, dst, send_sem, recv_sem, device):
        copy = remote(src, dst, send_sem, recv_sem, device)
        copy.start()
        copies.append(copy)
        return copy

    def got(dst, send_sem, recv_sem, device):
        remote(dst, dst, send_sem, recv_sem, device).wait_recv()

    loads = []
    for i, (src, dst) in enumerate(
        [(w_hbm, w_ref), (c_hbm, c_ref), (p_hbm, p_ref), (x_hbm, x_ref), (h_hbm, h_ref), (rv_hbm, rv_ref)]
    ):
        loads.append(pltpu.make_async_copy(src, dst, in_sem.at[i]))
        loads[i].start()

    barrier = pltpu.get_barrier_semaphore()
    for d in far_z:
        pl.semaphore_signal(barrier, inc=1, device_id={"row_0": plus_z(d)}, device_id_type=MESH)
    for d in far_x:
        pl.semaphore_signal(barrier, inc=1, device_id={"row_1": plus_x(d)}, device_id_type=MESH)
    pl.semaphore_signal(barrier, inc=1, device_id={"col": other}, device_id_type=MESH)

    loads[0].wait()
    loads[1].wait()
    direction = dot(w_ref[...], c_ref[half : 2 * half, :])
    loads[2].wait()
    direction = direction + dot(p_ref[...], c_ref[2 * half :, :])
    small_ref[2:4, :] = direction[:2, :]
    loads[3].wait()
    y_own[...] = direction + dot(x_ref[...], c_ref[:half, :])
    small_ref[0:2, :] = y_own[0:2, :]
    nb_tile[...] = jnp.zeros_like(nb_tile)
    for j in range(2):
        for q in range(2):
            row = 4 + j * 2 + q
            nb_tile[row : row + 1, :] = y_own[j : j + 1, q * LANES : (q + 1) * LANES]

    pl.semaphore_wait(barrier, nz + nx - 1)

    x_core = send(x_ref, x_par, cs_sem.at[0], cr_sem.at[0], {"col": other})
    y_core = send(y_own, y_par, cs_sem.at[1], cr_sem.at[1], {"col": other})
    for d in far_z:
        send(nb_tile, nb_all_z.at[z], nzs_sem.at[d], nzr_sem.at[z], {"row_0": plus_z(d)})

    def h_cols(which):
        tiles = half // LANES
        rows = []
        for j in range(2):
            rows.append(
                jnp.concatenate(
                    [h_ref[pl.ds((which * tiles + t) * 2 + j, owners, stride=8), :] for t in range(tiles)], axis=1
                )
            )
        return jnp.concatenate(rows, axis=0)

    def put(value, which):
        for j in range(2):
            for q in range(2):
                block = value[j * owners : (j + 1) * owners, q * LANES : (q + 1) * LANES]
                part[:, :, which * 4 + j * 2 + q, :] = block.reshape(nz, nx, LANES)

    loads[4].wait()
    loads[5].wait()
    h_own = h_cols(core)
    h_par = h_cols(other)
    hx = dot(h_own, x_ref[...])
    hy = dot(h_own, y_own[...])
    x_core.wait_recv()
    put(hx + dot(h_par, x_par[...]), 0)
    y_core.wait_recv()
    put(hy + dot(h_par, y_par[...]), 1)

    for k in far_pairs:
        first = 2 * pair_at(k)
        for d in far_x:
            send(
                part.at[pl.ds(first, 2), plus_x(d)],
                in_x.at[x, pl.ds(first, 2)],
                xs_sem.at[d, k],
                xr_sem.at[x, pair_at(k)],
                {"row_1": plus_x(d)},
            )

    def pack_pair(source, packed, pair):
        for low in range(2):
            packed[pair, low * 4 : (low + 1) * 4, :] = source[2 * pair + low, 4:8, :]

    nb_all_z[z] = nb_tile[...]
    for d in range(1, nz):
        s = plus_z(d)
        got(nb_all_z.at[s], nzs_sem.at[d], nzr_sem.at[s], {"row_0": s})
    for pair in range(pairs):
        pack_pair(nb_all_z, nb_pack, pair)
    nb_all_x[x] = nb_pack[...]
    for d in far_x:
        send(nb_pack, nb_all_x.at[x], nxs_sem.at[d], nxr_sem.at[x], {"row_1": plus_x(d)})

    for k in far_pairs:
        pair = pair_at(k)
        first = 2 * pair
        for d in range(1, nx):
            s = plus_x(d)
            got(in_x.at[s, pl.ds(first, 2)], xs_sem.at[d, k], xr_sem.at[s, pair], {"row_1": s})
        total = part[pl.ds(first, 2), x]
        for d in range(1, nx):
            total = total + in_x[plus_x(d), pl.ds(first, 2)]
        mid[pl.ds(first, 2)] = total
        if k:
            for low in range(2):
                to = first + low
                send(mid.at[to], in_z.at[z], zs_sem.at[2 * k + low], zr_sem.at[z], {"row_0": to})
        else:
            send(mid.at[z_mate], in_z.at[z], zs_sem.at[0], zr_sem.at[z], {"row_0": z_mate})

    own_sum = mid[z]
    for d in far_z:
        s = plus_z(d)
        got(in_z.at[s], zs_sem.at[d], zr_sem.at[s], {"row_0": s})
    for d in far_z:
        own_sum = own_sum + in_z[plus_z(d)]
    tile[...] = own_sum

    for q in range(2):
        squares = 0.0
        for j in range(2):
            columns = slice(q * LANES, (q + 1) * LANES)
            residual = tile[j * 2 + q : j * 2 + q + 1, :] - x_ref[j : j + 1, columns] * rv_ref[:, columns]
            small_ref[4 + j : 5 + j, columns] = residual
            squares = squares + residual * residual
        sq_own[q : q + 1, :] = squares
    tile[0:2, :] = sq_own[0:2, :]

    for d in far_z:
        send(tile, all_z.at[z], azs_sem.at[d], azr_sem.at[z], {"row_0": plus_z(d)})
    all_z[z] = tile[...]
    for k in near_pairs:
        pair = pair_at(k)
        for s in [2 * pair, 2 * pair + 1] if k else [z_mate]:
            got(all_z.at[s], azs_sem.at[0], azr_sem.at[s], {"row_0": s})
        pack_pair(all_z, pack, pair)
        for d in far_x:
            send(pack.at[pair], all_x.at[x, pair], axs_sem.at[d, k], axr_sem.at[x, pair], {"row_1": plus_x(d)})
    all_x[x] = pack[...]
    sq_tile[...] = jnp.sum(all_z[...], axis=0)
    for d in far_x:
        send(sq_tile, sq_all.at[x], qs_sem.at[d], qr_sem.at[x], {"row_1": plus_x(d)})
    sq_all[x] = sq_tile[...]

    def rows_of(source):
        columns = []
        for q in range(2):
            columns.append(
                jnp.concatenate(
                    [source[:, :, 2 * i + q, :].reshape(nx * pairs, LANES) for i in range(4)],
                    axis=0,
                )
            )
        return jnp.concatenate(columns, axis=1)

    for d in range(1, nx):
        s = plus_x(d)
        got(nb_all_x.at[s], nxs_sem.at[d], nxr_sem.at[s], {"row_1": s})
    nb_rows = rows_of(nb_all_x)
    core_own[0] = tdot(nb_rows, nb_rows)
    metric_core = send(core_own.at[0], core_par.at[0], cs_sem.at[2], cr_sem.at[2], {"col": other})

    for k in near_pairs:
        pair = pair_at(k)
        for d in range(1, nx):
            s = plus_x(d)
            got(all_x.at[s, pair], axs_sem.at[d, k], axr_sem.at[s, pair], {"row_1": s})
    core_own[1] = tdot(nb_rows, rows_of(all_x))
    ritz_core = send(core_own.at[1], core_par.at[1], cs_sem.at[4], cr_sem.at[4], {"col": other})

    for d in range(1, nx):
        s = plus_x(d)
        got(sq_all.at[s], qs_sem.at[d], qr_sem.at[s], {"row_1": s})
    sq_own[...] = jnp.sum(sq_all[...], axis=0)
    sq_core = send(sq_own, sq_par, cs_sem.at[3], cr_sem.at[3], {"col": other})
    metric_core.wait_recv()
    metric_ref[...] = core_own[0] + core_par[0]
    sq_core.wait_recv()
    for q in range(2):
        small_ref[6:7, q * LANES : (q + 1) * LANES] = sq_own[q : q + 1, :] + sq_par[q : q + 1, :]
    small_ref[7:8, :] = jnp.zeros((1, small_ref.shape[1]), jnp.float32)
    ritz_core.wait_recv()
    ritz_ref[...] = core_own[1] + core_par[1]

    for copy in copies:
        copy.wait_send()


def finish(window_total, small_in, ritz_in, metric_in, nb_ref, nd_ref, nc_ref, ritz_ref, metric_ref):
    ritz_ref[...] = ritz_in[...]
    metric_ref[...] = metric_in[...]
    nb_ref[...] = small_in[0:2, :]
    nd_ref[...] = small_in[2:4, :]
    nc_ref[...] = small_in[4:6, :] * lax.rsqrt(small_in[6:7, :] / window_total + 1e-06)


def on_device(hamiltonian_rows, current_block, correction_block, previous_block, ritz_values, mixing_coeffs):
    nz, nx = lax.axis_size("row_0"), lax.axis_size("row_1")
    pairs = nz // 2
    owners, _, out_rows, columns = hamiltonian_rows.shape
    block_width = current_block.shape[1]
    window_total = out_rows * owners * lax.axis_size("col")
    tiles = columns // LANES
    h_flat = hamiltonian_rows.reshape(owners, out_rows, tiles, LANES).transpose(0, 2, 1, 3)
    h_flat = h_flat.reshape(owners * tiles * out_rows, LANES)
    f32 = functools.partial(jax.ShapeDtypeStruct, dtype=jnp.float32)
    vmem = pl.BlockSpec(memory_space=pltpu.VMEM)
    hbm = pl.BlockSpec(memory_space=pltpu.HBM)
    square = (block_width, block_width)

    def buffer(*shape):
        return pltpu.VMEM(shape, jnp.float32)

    sems = pltpu.SemaphoreType.DMA
    sem_shapes = [
        (6,),
        (nx, pairs),
        (nx, pairs),
        (nz,),
        (nz,),
        (nz,),
        (nz,),
        (nx, pairs),
        (nx, pairs),
        (nx,),
        (nx,),
        (nz,),
        (nz,),
        (nx,),
        (nx,),
        (5,),
        (5,),
    ]
    small, ritz, metric = pl.pallas_call(
        functools.partial(kernel, nz, nx),
        out_shape=(f32((8, block_width)), f32(square), f32(square)),
        in_specs=[hbm] * 6,
        out_specs=(vmem,) * 3,
        scratch_shapes=[
            buffer(1, block_width),
            buffer(*h_flat.shape),
            buffer(*square),
            buffer(*square),
            buffer(*square),
            buffer(*mixing_coeffs.shape),
            buffer(*square),
            buffer(*square),
            buffer(*square),
            buffer(nz, nx, 8, LANES),
            buffer(nx, nz, 8, LANES),
            buffer(nz, 8, LANES),
            buffer(nz, 8, LANES),
            buffer(8, LANES),
            buffer(nz, 8, LANES),
            buffer(pairs, 8, LANES),
            buffer(nx, pairs, 8, LANES),
            buffer(8, LANES),
            buffer(nx, 8, LANES),
            buffer(8, LANES),
            buffer(nz, 8, LANES),
            buffer(pairs, 8, LANES),
            buffer(nx, pairs, 8, LANES),
            buffer(2, *square),
            buffer(2, *square),
            buffer(8, LANES),
            buffer(8, LANES),
        ]
        + [sems(shape) for shape in sem_shapes],
        compiler_params=pltpu.CompilerParams(
            collective_id=0, has_side_effects=True, vmem_limit_bytes=MAIN_VMEM
        ),
        name="lobpcg_step",
    )(
        *(
            pltpu.with_memory_space_constraint(a, pltpu.HBM)
            for a in (
                h_flat,
                current_block,
                correction_block,
                previous_block,
                mixing_coeffs,
                ritz_values.reshape(1, -1),
            )
        )
    )
    return pl.pallas_call(
        functools.partial(finish, window_total),
        out_shape=(f32((out_rows, block_width)),) * 3 + (f32(square),) * 2,
        in_specs=[vmem] * 3,
        out_specs=(vmem,) * 5,
        compiler_params=pltpu.CompilerParams(vmem_limit_bytes=END_VMEM),
        name="finish",
    )(small, ritz, metric)


def solution(mesh):
    finer = Mesh(
        mesh.devices.reshape(mesh.shape["chan"], NZ, NX, mesh.shape["col"]),
        ("chan", "row_0", "row_1", "col"),
    )
    in_specs = (
        P("chan", "col", None, ROW),
        P(CHAN_ROW_COL, None),
        P(CHAN_ROW_COL, None),
        P(CHAN_ROW_COL, None),
        P("chan"),
        P("chan", None),
    )
    out_specs = (
        P(CHAN_ROW_COL, None),
        P(CHAN_ROW_COL, None),
        P(CHAN_ROW_COL, None),
        P("chan", None),
        P("chan", None),
    )
    return jax.shard_map(on_device, mesh=finer, in_specs=in_specs, out_specs=out_specs, check_vma=False)
```

time: 101 us -> 89.2 us (0.88)
  Pallas kernels: 94.7 us -> 88.4 us
  local copies, waits for them, and re-layouts: 5 us -> 0 us
    pallas_call x1 -> x2, Pallas kernels: 94.7 us -> 88.4 us  [the longest x1 87.6 us: on_device(): pl.pallas_call(functools.partial(kernel, nz, nx), out_shape=(f32((8, bloc...]
    unnamed x13 -> x0, local copies, waits for them, and re-layouts: 5 us -> none
where the time goes in v2:
time: 89.2 us; the launch traced here: 89.1 us
  Pallas kernels  88.4 us (99%)
    pallas_call x1, Pallas kernels, on_device(): pl.pallas_call(functools.partial(kernel, nz, nx), out_shape=(f32((8, bloc...  87.6 us

profile of v2, /device:TPU:65, one launch (start us, length us, event | category | flops | bytes accessed | tf_op | source)
XLA Modules:
  0.0 89.1 jit_solution(571541794968378685)
XLA Ops:
  0.6 87.6 %lobpcg_step.1 = (f32[8,256]{1,0:T(8,128)S(1)}, f32[256,256]{1,0:T(8,128)S(1)}, f32[256,256]{1,0:T(8,128)S(1)}) custom-call(f32[1024,128]{1,0:T(8,128)} %bitcast.6, f32[256,256]{1,0:T(8,128)} %x_hbm.1, f32[256,256]{1,0:T(8,128)} %w_hbm.1, f32[256,256]{1,0:T(8,128)} %p_hbm.1, f32[768,256]{1,0:T(8,128)} %c_hbm.1, f32[1,256]{1,0:T(1,128)} %bitcast.7), custom_call_target="tpu_custom_call" | custom-call | tf_op jit(solution)/shard_map/lobpcg_step/pallas_call | solution.py:360
  88.2 0.8 finish.1

commit v3 on v2

--- a/solution.py
+++ b/solution.py
@@ -53,19 +53,28 @@
     y_own,
     x_par,
     y_par,
-    part,
+    part_x,
+    part_y,
     in_x,
-    mid,
-    in_z,
-    tile,
-    all_z,
-    pack,
-    all_x,
+    in_y,
+    hop_in_x,
+    hop_in_y,
+    hop_x,
+    hop_y,
+    mid_x,
+    mid_y,
+    in_xz,
+    in_yz,
+    tile_x,
+    tile_y,
+    y_all_z,
+    y_all_x,
     sq_tile,
-    sq_all,
+    sq_all_z,
+    sq_sum,
+    sq_all_x,
     nb_tile,
     nb_all_z,
-    nb_pack,
     nb_all_x,
     core_own,
     core_par,
@@ -74,14 +83,24 @@
     in_sem,
     xs_sem,
     xr_sem,
-    zs_sem,
-    zr_sem,
-    azs_sem,
-    azr_sem,
-    axs_sem,
-    axr_sem,
-    qs_sem,
-    qr_sem,
+    ys_sem,
+    yr_sem,
+    hxs_sem,
+    hxr_sem,
+    hys_sem,
+    hyr_sem,
+    xzs_sem,
+    xzr_sem,
+    yzs_sem,
+    yzr_sem,
+    gzs_sem,
+    gzr_sem,
+    gxs_sem,
+    gxr_sem,
+    qzs_sem,
+    qzr_sem,
+    qxs_sem,
+    qxr_sem,
     nzs_sem,
     nzr_sem,
     nxs_sem,
@@ -96,10 +115,12 @@
     owners = nz * nx
     pairs = nz // 2
     half = x_ref.shape[0]
+    opposite = nx // 2
     own_pair = z // 2
     z_mate = 2 * own_pair + 1 - lax.rem(z, 2)
     far_z = sorted(range(1, nz), key=lambda d: -min(d, nz - d))
     far_x = sorted(range(1, nx), key=lambda d: -min(d, nx - d))
+    near_x = [d for d in far_x if d != opposite]
     far_pairs = sorted(range(pairs), key=lambda k: -min(k, pairs - k))
     near_pairs = far_pairs[::-1]
 
@@ -107,10 +128,13 @@
         return lax.rem(z + d, nz)
 
     def plus_x(d):
-        return lax.rem(x + d, nx)
+        return lax.rem(x + d % nx, nx)
 
     def pair_at(k):
         return lax.rem(own_pair + k, pairs)
+
+    def way(k):
+        return 1 if k % 2 == 0 else -1
 
     def remote(src, dst, send, recv, device):
         return pltpu.make_async_remote_copy(
@@ -151,16 +175,14 @@
     loads[3].wait()
     y_own[...] = direction + dot(x_ref[...], c_ref[:half, :])
     small_ref[0:2, :] = y_own[0:2, :]
-    nb_tile[...] = jnp.zeros_like(nb_tile)
     for j in range(2):
         for q in range(2):
-            row = 4 + j * 2 + q
-            nb_tile[row : row + 1, :] = y_own[j : j + 1, q * LANES : (q + 1) * LANES]
+            nb_tile[j * 2 + q : j * 2 + q + 1, :] = y_own[j : j + 1, q * LANES : (q + 1) * LANES]
 
     pl.semaphore_wait(barrier, nz + nx - 1)
 
+    y_core = send(y_own, y_par, cs_sem.at[1], cr_sem.at[1], {"col": other})
     x_core = send(x_ref, x_par, cs_sem.at[0], cr_sem.at[0], {"col": other})
-    y_core = send(y_own, y_par, cs_sem.at[1], cr_sem.at[1], {"col": other})
     for d in far_z:
         send(nb_tile, nb_all_z.at[z], nzs_sem.at[d], nzr_sem.at[z], {"row_0": plus_z(d)})
 
@@ -175,136 +197,198 @@
             )
         return jnp.concatenate(rows, axis=0)
 
-    def put(value, which):
+    def put(value, part):
         for j in range(2):
             for q in range(2):
                 block = value[j * owners : (j + 1) * owners, q * LANES : (q + 1) * LANES]
-                part[:, :, which * 4 + j * 2 + q, :] = block.reshape(nz, nx, LANES)
-
+                part[:, :, j * 2 + q, :] = block.reshape(nz, nx, LANES)
+
+    def send_chunk(part, into, s_sem, r_sem, k, d):
+        pair = pair_at(k)
+        send(
+            part.at[pl.ds(2 * pair, 2), plus_x(d)],
+            into.at[x, pl.ds(2 * pair, 2)],
+            s_sem.at[d % nx, k],
+            r_sem.at[x, pair],
+            {"row_1": plus_x(d)},
+        )
+
+    def start_sum(part, into, s_sem, r_sem, hop_in, hs_sem, hr_sem):
+        for k in far_pairs:
+            send(
+                part.at[pl.ds(2 * pair_at(k), 2), plus_x(opposite)],
+                hop_in.at[k],
+                hs_sem.at[k],
+                hr_sem.at[k],
+                {"row_1": plus_x(way(k))},
+            )
+        for k in far_pairs:
+            for d in near_x:
+                if d != way(k) * (opposite - 1) % nx:
+                    send_chunk(part, into, s_sem, r_sem, k, d)
+
+    def hop_on(part, into, s_sem, r_sem, hop_in, hop, hs_sem, hr_sem):
+        for k in far_pairs:
+            pair = pair_at(k)
+            d = way(k) * (opposite - 1)
+            got(hop_in.at[k], hs_sem.at[k], hr_sem.at[k], {"row_1": plus_x(-way(k))})
+            hop[k] = hop_in[k] + part[pl.ds(2 * pair, 2), plus_x(d)]
+            send(
+                hop.at[k],
+                into.at[x, pl.ds(2 * pair, 2)],
+                s_sem.at[d % nx, k],
+                r_sem.at[x, pair],
+                {"row_1": plus_x(d)},
+            )
+
+    def sum_pairs(part, into, s_sem, r_sem, mid, into_z, zs_sem, zr_sem):
+        for k in far_pairs:
+            pair = pair_at(k)
+            first = 2 * pair
+            for d in near_x:
+                s = plus_x(d)
+                got(into.at[s, pl.ds(first, 2)], s_sem.at[d, k], r_sem.at[s, pair], {"row_1": s})
+            total = part[pl.ds(first, 2), x]
+            for d in near_x:
+                total = total + into[plus_x(d), pl.ds(first, 2)]
+            mid[pl.ds(first, 2)] = total
+            if k:
+                for low in range(2):
+                    to = first + low
+                    send(mid.at[to], into_z.at[z], zs_sem.at[2 * k + low], zr_sem.at[z], {"row_0": to})
+            else:
+                send(mid.at[z_mate], into_z.at[z], zs_sem.at[0], zr_sem.at[z], {"row_0": z_mate})
+
+    def sum_z(mid, into_z, zs_sem, zr_sem):
+        for d in far_z:
+            s = plus_z(d)
+            got(into_z.at[s], zs_sem.at[d], zr_sem.at[s], {"row_0": s})
+        total = mid[z]
+        for d in far_z:
+            total = total + into_z[plus_z(d)]
+        return total
+
+    y_sum = (part_y, in_y, ys_sem, yr_sem)
+    x_sum = (part_x, in_x, xs_sem, xr_sem)
     loads[4].wait()
     loads[5].wait()
     h_own = h_cols(core)
     h_par = h_cols(other)
+    hy = dot(h_own, y_own[...])
+    y_core.wait_recv()
+    put(hy + dot(h_par, y_par[...]), part_y)
+    start_sum(*y_sum, hop_in_y, hys_sem, hyr_sem)
     hx = dot(h_own, x_ref[...])
-    hy = dot(h_own, y_own[...])
     x_core.wait_recv()
-    put(hx + dot(h_par, x_par[...]), 0)
-    y_core.wait_recv()
-    put(hy + dot(h_par, y_par[...]), 1)
-
-    for k in far_pairs:
-        first = 2 * pair_at(k)
-        for d in far_x:
-            send(
-                part.at[pl.ds(first, 2), plus_x(d)],
-                in_x.at[x, pl.ds(first, 2)],
-                xs_sem.at[d, k],
-                xr_sem.at[x, pair_at(k)],
-                {"row_1": plus_x(d)},
-            )
-
-    def pack_pair(source, packed, pair):
-        for low in range(2):
-            packed[pair, low * 4 : (low + 1) * 4, :] = source[2 * pair + low, 4:8, :]
+    put(hx + dot(h_par, x_par[...]), part_x)
+    hop_on(*y_sum, hop_in_y, hop_y, hys_sem, hyr_sem)
+    start_sum(*x_sum, hop_in_x, hxs_sem, hxr_sem)
+    sum_pairs(*y_sum, mid_y, in_yz, yzs_sem, yzr_sem)
+    hop_on(*x_sum, hop_in_x, hop_x, hxs_sem, hxr_sem)
+
+    tile_y[...] = sum_z(mid_y, in_yz, yzs_sem, yzr_sem)
+    for d in far_z:
+        send(tile_y, y_all_z.at[z], gzs_sem.at[d], gzr_sem.at[z], {"row_0": plus_z(d)})
+    y_all_z[z] = tile_y[...]
+
+    def ring(step):
+        for sign in (1, -1):
+            if step <= opposite - (sign < 0):
+                s = plus_x(-sign * (step - 1))
+                slot = sign * step % nx
+                if step > 1:
+                    got(nb_all_x.at[s], nxs_sem.at[slot], nxr_sem.at[s], {"row_1": s})
+                send(
+                    nb_all_x.at[s] if step > 1 else nb_all_z,
+                    nb_all_x.at[s],
+                    nxs_sem.at[slot],
+                    nxr_sem.at[s],
+                    {"row_1": plus_x(sign)},
+                )
 
     nb_all_z[z] = nb_tile[...]
     for d in range(1, nz):
         s = plus_z(d)
         got(nb_all_z.at[s], nzs_sem.at[d], nzr_sem.at[s], {"row_0": s})
-    for pair in range(pairs):
-        pack_pair(nb_all_z, nb_pack, pair)
-    nb_all_x[x] = nb_pack[...]
-    for d in far_x:
-        send(nb_pack, nb_all_x.at[x], nxs_sem.at[d], nxr_sem.at[x], {"row_1": plus_x(d)})
-
-    for k in far_pairs:
-        pair = pair_at(k)
-        first = 2 * pair
-        for d in range(1, nx):
-            s = plus_x(d)
-            got(in_x.at[s, pl.ds(first, 2)], xs_sem.at[d, k], xr_sem.at[s, pair], {"row_1": s})
-        total = part[pl.ds(first, 2), x]
-        for d in range(1, nx):
-            total = total + in_x[plus_x(d), pl.ds(first, 2)]
-        mid[pl.ds(first, 2)] = total
-        if k:
-            for low in range(2):
-                to = first + low
-                send(mid.at[to], in_z.at[z], zs_sem.at[2 * k + low], zr_sem.at[z], {"row_0": to})
-        else:
-            send(mid.at[z_mate], in_z.at[z], zs_sem.at[0], zr_sem.at[z], {"row_0": z_mate})
-
-    own_sum = mid[z]
-    for d in far_z:
-        s = plus_z(d)
-        got(in_z.at[s], zs_sem.at[d], zr_sem.at[s], {"row_0": s})
-    for d in far_z:
-        own_sum = own_sum + in_z[plus_z(d)]
-    tile[...] = own_sum
-
+    ring(1)
+    nb_all_x[x] = nb_all_z[...]
+
+    sum_pairs(*x_sum, mid_x, in_xz, xzs_sem, xzr_sem)
+    ring(2)
+    tile_x[...] = sum_z(mid_x, in_xz, xzs_sem, xzr_sem)
     for q in range(2):
         squares = 0.0
         for j in range(2):
             columns = slice(q * LANES, (q + 1) * LANES)
-            residual = tile[j * 2 + q : j * 2 + q + 1, :] - x_ref[j : j + 1, columns] * rv_ref[:, columns]
+            residual = tile_x[j * 2 + q : j * 2 + q + 1, :] - x_ref[j : j + 1, columns] * rv_ref[:, columns]
             small_ref[4 + j : 5 + j, columns] = residual
             squares = squares + residual * residual
-        sq_own[q : q + 1, :] = squares
-    tile[0:2, :] = sq_own[0:2, :]
-
+        sq_tile[q : q + 1, :] = squares
     for d in far_z:
-        send(tile, all_z.at[z], azs_sem.at[d], azr_sem.at[z], {"row_0": plus_z(d)})
-    all_z[z] = tile[...]
+        send(sq_tile, sq_all_z.at[z], qzs_sem.at[d], qzr_sem.at[z], {"row_0": plus_z(d)})
+    sq_all_z[z] = sq_tile[...]
+    ring(3)
+
     for k in near_pairs:
         pair = pair_at(k)
         for s in [2 * pair, 2 * pair + 1] if k else [z_mate]:
-            got(all_z.at[s], azs_sem.at[0], azr_sem.at[s], {"row_0": s})
-        pack_pair(all_z, pack, pair)
+            got(y_all_z.at[s], gzs_sem.at[0], gzr_sem.at[s], {"row_0": s})
+        pair_slice = pl.ds(2 * pair, 2)
         for d in far_x:
-            send(pack.at[pair], all_x.at[x, pair], axs_sem.at[d, k], axr_sem.at[x, pair], {"row_1": plus_x(d)})
-    all_x[x] = pack[...]
-    sq_tile[...] = jnp.sum(all_z[...], axis=0)
-    for d in far_x:
-        send(sq_tile, sq_all.at[x], qs_sem.at[d], qr_sem.at[x], {"row_1": plus_x(d)})
-    sq_all[x] = sq_tile[...]
+            send(
+                y_all_z.at[pair_slice],
+                y_all_x.at[x, pair_slice],
+                gxs_sem.at[d, k],
+                gxr_sem.at[x, pair],
+                {"row_1": plus_x(d)},
+            )
+    y_all_x[x] = y_all_z[...]
 
     def rows_of(source):
         columns = []
         for q in range(2):
             columns.append(
-                jnp.concatenate(
-                    [source[:, :, 2 * i + q, :].reshape(nx * pairs, LANES) for i in range(4)],
-                    axis=0,
-                )
+                jnp.concatenate([source[:, :, 2 * j + q, :].reshape(owners, LANES) for j in range(2)], axis=0)
             )
         return jnp.concatenate(columns, axis=1)
 
-    for d in range(1, nx):
-        s = plus_x(d)
-        got(nb_all_x.at[s], nxs_sem.at[d], nxr_sem.at[s], {"row_1": s})
+    for step in range(4, opposite + 1):
+        ring(step)
+    ends = {opposite, 1 - opposite} if opposite > 1 else {1}
+    for d in sorted(ends):
+        s = plus_x(-d)
+        got(nb_all_x.at[s], nxs_sem.at[0], nxr_sem.at[s], {"row_1": s})
     nb_rows = rows_of(nb_all_x)
     core_own[0] = tdot(nb_rows, nb_rows)
     metric_core = send(core_own.at[0], core_par.at[0], cs_sem.at[2], cr_sem.at[2], {"col": other})
+
+    for d in far_z:
+        s = plus_z(d)
+        got(sq_all_z.at[s], qzs_sem.at[d], qzr_sem.at[s], {"row_0": s})
+    sq_sum[...] = jnp.sum(sq_all_z[...], axis=0)
+    for d in far_x:
+        send(sq_sum, sq_all_x.at[x], qxs_sem.at[d], qxr_sem.at[x], {"row_1": plus_x(d)})
+    sq_all_x[x] = sq_sum[...]
 
     for k in near_pairs:
         pair = pair_at(k)
         for d in range(1, nx):
             s = plus_x(d)
-            got(all_x.at[s, pair], axs_sem.at[d, k], axr_sem.at[s, pair], {"row_1": s})
-    core_own[1] = tdot(nb_rows, rows_of(all_x))
+            got(y_all_x.at[s, pl.ds(2 * pair, 2)], gxs_sem.at[d, k], gxr_sem.at[s, pair], {"row_1": s})
+    core_own[1] = tdot(nb_rows, rows_of(y_all_x))
     ritz_core = send(core_own.at[1], core_par.at[1], cs_sem.at[4], cr_sem.at[4], {"col": other})
 
     for d in range(1, nx):
         s = plus_x(d)
-        got(sq_all.at[s], qs_sem.at[d], qr_sem.at[s], {"row_1": s})
-    sq_own[...] = jnp.sum(sq_all[...], axis=0)
+        got(sq_all_x.at[s], qxs_sem.at[d], qxr_sem.at[s], {"row_1": s})
+    sq_own[...] = jnp.sum(sq_all_x[...], axis=0)
     sq_core = send(sq_own, sq_par, cs_sem.at[3], cr_sem.at[3], {"col": other})
     metric_core.wait_recv()
     metric_ref[...] = core_own[0] + core_par[0]
+    small_ref[7:8, :] = jnp.zeros((1, small_ref.shape[1]), jnp.float32)
     sq_core.wait_recv()
     for q in range(2):
         small_ref[6:7, q * LANES : (q + 1) * LANES] = sq_own[q : q + 1, :] + sq_par[q : q + 1, :]
-    small_ref[7:8, :] = jnp.zeros((1, small_ref.shape[1]), jnp.float32)
     ritz_core.wait_recv()
     ritz_ref[...] = core_own[1] + core_par[1]
 
@@ -338,25 +422,19 @@
         return pltpu.VMEM(shape, jnp.float32)
 
     sems = pltpu.SemaphoreType.DMA
-    sem_shapes = [
-        (6,),
-        (nx, pairs),
-        (nx, pairs),
-        (nz,),
-        (nz,),
-        (nz,),
-        (nz,),
-        (nx, pairs),
-        (nx, pairs),
-        (nx,),
-        (nx,),
-        (nz,),
-        (nz,),
-        (nx,),
-        (nx,),
-        (5,),
-        (5,),
-    ]
+    sem_shapes = (
+        [(6,)]
+        + [(nx, pairs)] * 4
+        + [(pairs,)] * 4
+        + [(nz,)] * 6
+        + [(nx, pairs)] * 2
+        + [(nz,)] * 2
+        + [(nx,)] * 2
+        + [(nz,)] * 2
+        + [(nx,)] * 2
+        + [(5,)] * 2
+    )
+    chunk = (4, LANES)
     small, ritz, metric = pl.pallas_call(
         functools.partial(kernel, nz, nx),
         out_shape=(f32((8, block_width)), f32(square), f32(square)),
@@ -372,24 +450,33 @@
             buffer(*square),
             buffer(*square),
             buffer(*square),
-            buffer(nz, nx, 8, LANES),
-            buffer(nx, nz, 8, LANES),
-            buffer(nz, 8, LANES),
-            buffer(nz, 8, LANES),
-            buffer(8, LANES),
-            buffer(nz, 8, LANES),
-            buffer(pairs, 8, LANES),
-            buffer(nx, pairs, 8, LANES),
-            buffer(8, LANES),
-            buffer(nx, 8, LANES),
-            buffer(8, LANES),
-            buffer(nz, 8, LANES),
-            buffer(pairs, 8, LANES),
-            buffer(nx, pairs, 8, LANES),
+            buffer(nz, nx, *chunk),
+            buffer(nz, nx, *chunk),
+            buffer(nx, nz, *chunk),
+            buffer(nx, nz, *chunk),
+            buffer(pairs, 2, *chunk),
+            buffer(pairs, 2, *chunk),
+            buffer(pairs, 2, *chunk),
+            buffer(pairs, 2, *chunk),
+            buffer(nz, *chunk),
+            buffer(nz, *chunk),
+            buffer(nz, *chunk),
+            buffer(nz, *chunk),
+            buffer(*chunk),
+            buffer(*chunk),
+            buffer(nz, *chunk),
+            buffer(nx, nz, *chunk),
+            buffer(2, LANES),
+            buffer(nz, 2, LANES),
+            buffer(2, LANES),
+            buffer(nx, 2, LANES),
+            buffer(*chunk),
+            buffer(nz, *chunk),
+            buffer(nx, nz, *chunk),
             buffer(2, *square),
             buffer(2, *square),
-            buffer(8, LANES),
-            buffer(8, LANES),
+            buffer(2, LANES),
+            buffer(2, LANES),
         ]
         + [sems(shape) for shape in sem_shapes],
         compiler_params=pltpu.CompilerParams(

time: 89.2 us -> 94.8 us (1.063)
  Pallas kernels: 88.4 us -> 94 us
    pallas_call x1, Pallas kernels: 87.6 us -> 93.2 us  [on_device(): pl.pallas_call(functools.partial(kernel, nz, nx), out_shape=(f32((8, bloc...]
where the time goes in v3:
time: 94.8 us; the launch traced here: 94.6 us
  Pallas kernels  94 us (99%)
    pallas_call x1, Pallas kernels, on_device(): pl.pallas_call(functools.partial(kernel, nz, nx), out_shape=(f32((8, bloc...  93.2 us

profile of v3, /device:TPU:65, one launch (start us, length us, event | category | flops | bytes accessed | tf_op | source)
XLA Modules:
  0.0 94.6 jit_solution(13539261087586672977)
XLA Ops:
  0.6 93.2 %lobpcg_step.1 = (f32[8,256]{1,0:T(8,128)S(1)}, f32[256,256]{1,0:T(8,128)S(1)}, f32[256,256]{1,0:T(8,128)S(1)}) custom-call(f32[1024,128]{1,0:T(8,128)} %bitcast.6, f32[256,256]{1,0:T(8,128)} %x_hbm.1, f32[256,256]{1,0:T(8,128)} %w_hbm.1, f32[256,256]{1,0:T(8,128)} %p_hbm.1, f32[768,256]{1,0:T(8,128)} %c_hbm.1, f32[1,256]{1,0:T(1,128)} %bitcast.7), custom_call_target="tpu_custom_call" | custom-call | tf_op jit(solution)/shard_map/lobpcg_step/pallas_call | solution.py:438
  93.8 0.8 finish.1

commit v4 on v2

v4 whole, which is shorter than its diff:
```python
import functools

import jax
import jax.numpy as jnp
from jax import lax
from jax.experimental import pallas as pl
from jax.experimental.pallas import tpu as pltpu
from jax.sharding import Mesh
from jax.sharding import PartitionSpec as P

NZ, NX = 16, 8
ROW = ("row_0", "row_1")
CHAN_ROW_COL = ("chan", "row_0", "row_1", "col")
MESH = pl.DeviceIdType.MESH
LANES = 128
GROUP = 4
MAIN_VMEM = 24 * 2**20
END_VMEM = 8 * 2**20
HIGHEST = lax.Precision.HIGHEST


def dot(left, right):
    return jnp.dot(left, right, preferred_element_type=jnp.float32, precision=HIGHEST)


def tdot(left, right):
    return lax.dot_general(
        left,
        right,
        (((0,), (0,)), ((), ())),
        preferred_element_type=jnp.float32,
        precision=HIGHEST,
    )


def kernel(
    nz,
    nx,
    h_hbm,
    x_hbm,
    w_hbm,
    p_hbm,
    c_hbm,
    rv_hbm,
    small_ref,
    ritz_ref,
    metric_ref,
    rv_ref,
    h_ref,
    c_ref,
    rows,
    h_rows,
    prod,
    part,
    in_x,
    mid,
    in_z,
    tile,
    all_z,
    gathered,
    nb_tile,
    nb_all_z,
    nb_t,
    sq_tile,
    sq_all_z,
    sq_sum,
    sq_all_x,
    core_own,
    core_par,
    sq_own,
    sq_par,
    in_sem,
    xs_sem,
    xr_sem,
    zs_sem,
    zr_sem,
    gzs_sem,
    gzr_sem,
    gxs_sem,
    gxr_sem,
    qzs_sem,
    qzr_sem,
    qxs_sem,
    qxr_sem,
    nzs_sem,
    nzr_sem,
    nxs_sem,
    nxr_sem,
    cs_sem,
    cr_sem,
):
    z = lax.axis_index("row_0")
    x = lax.axis_index("row_1")
    core = lax.axis_index("col")
    other = 1 - core
    owners = nz * nx
    groups = nz // GROUP
    own_group = z // GROUP
    half = rows.shape[1]

    def plus_z(d):
        return lax.rem(z + d, nz)

    def plus_x(d):
        return lax.rem(x + d, nx)

    def far_group(k):
        step = (k + 1) // 2
        return lax.rem(own_group + groups // 2 + step * (1 - 2 * lax.rem(k, 2)) + groups, groups)

    def member(group, m):
        return group * GROUP + lax.rem(lax.rem(z, GROUP) + m, GROUP)

    def remote(src, dst, send, recv, device):
        return pltpu.make_async_remote_copy(
            src_ref=src, dst_ref=dst, send_sem=send, recv_sem=recv, device_id=device, device_id_type=MESH
        )

    def loop(first, last, body):
        def step(i, carry):
            body(i)
            return carry

        lax.fori_loop(first, last, step, 0)

    def send_all_z(src, into, s_sem, r_sem):
        loop(1, nz, lambda d: remote(src, into.at[z], s_sem.at[d], r_sem.at[z], {"row_0": plus_z(d)}).start())

    def got_all_z(into, s_sem, r_sem):
        loop(1, nz, lambda d: remote(into.at[z], into.at[z], s_sem.at[d], r_sem.at[plus_z(d)], {"row_0": z}).wait_recv())

    def sent_all_z(src, s_sem, r_sem):
        loop(1, nz, lambda d: remote(src, src, s_sem.at[d], r_sem.at[z], {"row_0": z}).wait_send())

    def send_all_x(src, into, s_sem, r_sem):
        loop(1, nx, lambda d: remote(src, into.at[x], s_sem.at[d], r_sem.at[x], {"row_1": plus_x(d)}).start())

    def got_all_x(into, s_sem, r_sem):
        loop(1, nx, lambda d: remote(into.at[x], into.at[x], s_sem.at[d], r_sem.at[plus_x(d)], {"row_1": x}).wait_recv())

    def sent_all_x(src, s_sem, r_sem):
        loop(1, nx, lambda d: remote(src, src, s_sem.at[d], r_sem.at[x], {"row_1": x}).wait_send())

    def core_copy(src, dst, i):
        return remote(src, dst, cs_sem.at[i], cr_sem.at[i], {"col": other})

    loads = []
    for i, (src, dst) in enumerate(
        [
            (w_hbm, rows.at[0]),
            (c_hbm.at[pl.ds(half, half)], c_ref.at[0]),
            (p_hbm, rows.at[1]),
            (c_hbm.at[pl.ds(2 * half, half)], c_ref.at[1]),
            (x_hbm, rows.at[2]),
            (c_hbm.at[pl.ds(0, half)], c_ref.at[2]),
            (h_hbm, h_ref),
            (rv_hbm, rv_ref),
        ]
    ):
        loads.append(pltpu.make_async_copy(src, dst, in_sem.at[i]))
        loads[i].start()

    barrier = pltpu.get_barrier_semaphore()
    loop(1, nz, lambda d: pl.semaphore_signal(barrier, inc=1, device_id={"row_0": plus_z(d)}, device_id_type=MESH))
    loop(1, nx, lambda d: pl.semaphore_signal(barrier, inc=1, device_id={"row_1": plus_x(d)}, device_id_type=MESH))
    pl.semaphore_signal(barrier, inc=1, device_id={"col": other}, device_id_type=MESH)

    for load in loads[:6]:
        load.wait()

    rows[4] = jnp.zeros(rows.shape[1:], jnp.float32)

    def add_product(i):
        small_ref[2:4, :] = rows[4, 0:2, :]
        rows[4] += dot(rows[i], c_ref[i])

    loop(0, 3, add_product)
    small_ref[0:2, :] = rows[4, 0:2, :]
    for j in range(2):
        for q in range(2):
            nb_tile[j * 2 + q : j * 2 + q + 1, :] = rows[4, j : j + 1, q * LANES : (q + 1) * LANES]

    pl.semaphore_wait(barrier, nz + nx - 1)
    y_core = core_copy(rows.at[4], rows.at[5], 1)
    y_core.start()
    x_core = core_copy(rows.at[2], rows.at[3], 0)
    x_core.start()
    send_all_z(nb_tile, nb_all_z, nzs_sem, nzr_sem)

    loads[6].wait()
    loads[7].wait()
    tiles = half // LANES

    def order(n):
        i = n // nx
        owner_x = lax.rem(n, nx)
        which = core + i - 2 * core * i
        for j in range(2):
            to = pl.multiple_of(j * owners + owner_x * nz, nz)
            for t in range(tiles):
                h_rows[i, pl.ds(to, nz), t * LANES : (t + 1) * LANES] = h_ref[
                    pl.ds(owner_x * 8 + (which * tiles + t) * 2 + j, nz, stride=8 * nx), :
                ]

    loop(0, 2 * nx, order)

    def own_product(v):
        prod[v] = dot(h_rows[0], rows[4 - 2 * v])

    loop(0, 2, own_product)
    y_core.wait_recv()
    x_core.wait_recv()

    def other_product(v):
        value = prod[v] + dot(h_rows[1], rows[5 - 2 * v])
        for j in range(2):
            for q in range(2):
                block = value[j * owners : (j + 1) * owners, q * LANES : (q + 1) * LANES]
                part[v, :, :, j * 2 + q, :] = block.reshape(nx, nz, LANES)

        def send_group(k):
            group = far_group(k)
            members = pl.ds(group * GROUP, GROUP)
            loop(
                1,
                nx,
                lambda d: remote(
                    part.at[v, plus_x(d), members],
                    in_x.at[v, x, members],
                    xs_sem.at[v, group, d],
                    xr_sem.at[v, group, x],
                    {"row_1": plus_x(d)},
                ).start(),
            )

        loop(0, groups, send_group)

    loop(0, 2, other_product)

    def pass_group(n):
        v = n // groups
        k = lax.rem(n, groups)
        group = far_group(k)
        members = pl.ds(group * GROUP, GROUP)
        own = part.at[v, x, members]
        loop(
            1,
            nx,
            lambda d: remote(
                own, in_x.at[v, x, members], xs_sem.at[v, group, d], xr_sem.at[v, group, plus_x(d)], {"row_1": x}
            ).wait_recv(),
        )
        total = part[v, x, members]
        for d in range(1, nx):
            total = total + in_x[v, plus_x(d), members]
        mid[v, members] = total

        def send_member(m):
            to = member(group, m)
            remote(mid.at[v, to], in_z.at[v, z], zs_sem.at[v, to], zr_sem.at[v, z], {"row_0": to}).start()

        @pl.when(k < groups - 1)
        def _():
            send_member(0)

        loop(1, GROUP, send_member)

    loop(0, 2 * groups, pass_group)

    def sum_z(v):
        loop(
            1,
            nz,
            lambda d: remote(
                mid.at[v, z], in_z.at[v, z], zs_sem.at[v, z], zr_sem.at[v, plus_z(d)], {"row_0": z}
            ).wait_recv(),
        )
        total = mid[v, z]
        for d in range(1, nz):
            total = total + in_z[v, plus_z(d)]
        tile[v] = total

    sum_z(0)
    send_all_z(tile.at[0], all_z, gzs_sem, gzr_sem)
    all_z[z] = tile[0]

    got_all_z(nb_all_z, nzs_sem, nzr_sem)
    nb_all_z[z] = nb_tile[...]
    send_all_x(nb_all_z, gathered.at[0], nxs_sem, nxr_sem)
    gathered[0, x] = nb_all_z[...]

    sum_z(1)
    for q in range(2):
        squares = 0.0
        for j in range(2):
            columns = slice(q * LANES, (q + 1) * LANES)
            residual = tile[1, j * 2 + q : j * 2 + q + 1, :] - rows[2, j : j + 1, columns] * rv_ref[:, columns]
            small_ref[4 + j : 5 + j, columns] = residual
            squares = squares + residual * residual
        sq_tile[q : q + 1, :] = squares
    send_all_z(sq_tile, sq_all_z, qzs_sem, qzr_sem)
    sq_all_z[z] = sq_tile[...]

    def forward(n):
        k = groups - 1 - n
        group = far_group(k)
        members = pl.ds(group * GROUP, GROUP)

        def got_member(m):
            s = member(group, m)
            remote(all_z.at[s], all_z.at[s], gzs_sem.at[0], gzr_sem.at[s], {"row_0": z}).wait_recv()

        @pl.when(k < groups - 1)
        def _():
            got_member(0)

        loop(1, GROUP, got_member)
        loop(
            1,
            nx,
            lambda d: remote(
                all_z.at[members],
                gathered.at[1, x, members],
                gxs_sem.at[group, d],
                gxr_sem.at[group, x],
                {"row_1": plus_x(d)},
            ).start(),
        )

    loop(0, groups, forward)
    gathered[1, x] = all_z[...]

    def rows_of(u):
        columns = []
        for q in range(2):
            columns.append(
                jnp.concatenate([gathered[u, :, :, 2 * j + q, :].reshape(owners, LANES) for j in range(2)], axis=0)
            )
        return jnp.concatenate(columns, axis=1)

    got_all_x(gathered.at[0], nxs_sem, nxr_sem)
    nb_t[...] = rows_of(0).T

    def last_product(u):
        @pl.when(u == 1)
        def _():
            got_all_z(sq_all_z, qzs_sem, qzr_sem)
            sq_sum[...] = jnp.sum(sq_all_z[...], axis=0)
            send_all_x(sq_sum, sq_all_x, qxs_sem, qxr_sem)
            sq_all_x[x] = sq_sum[...]

            def got_group(group):
                members = pl.ds(group * GROUP, GROUP)
                loop(
                    1,
                    nx,
                    lambda d: remote(
                        all_z.at[members],
                        gathered.at[1, x, members],
                        gxs_sem.at[group, d],
                        gxr_sem.at[group, plus_x(d)],
                        {"row_1": x},
                    ).wait_recv(),
                )

            loop(0, groups, got_group)

        core_own[u] = dot(nb_t[...], rows_of(u))
        remote(core_own.at[u], core_par.at[u], cs_sem.at[2 + u], cr_sem.at[2 + u], {"col": other}).start()

    loop(0, 2, last_product)

    got_all_x(sq_all_x, qxs_sem, qxr_sem)
    sq_own[...] = jnp.sum(sq_all_x[...], axis=0)
    sq_core = core_copy(sq_own, sq_par, 4)
    sq_core.start()
    core_copy(core_own.at[0], core_par.at[0], 2).wait_recv()
    metric_ref[...] = core_own[0] + core_par[0]
    small_ref[7:8, :] = jnp.zeros((1, small_ref.shape[1]), jnp.float32)
    sq_core.wait_recv()
    for q in range(2):
        small_ref[6:7, q * LANES : (q + 1) * LANES] = sq_own[q : q + 1, :] + sq_par[q : q + 1, :]

    y_core.wait_send()
    x_core.wait_send()
    sent_all_z(nb_tile, nzs_sem, nzr_sem)
    sent_all_z(tile.at[0], gzs_sem, gzr_sem)
    sent_all_z(sq_tile, qzs_sem, qzr_sem)
    sent_all_x(nb_all_z, nxs_sem, nxr_sem)
    sent_all_x(sq_sum, qxs_sem, qxr_sem)

    def sent_sums(n):
        v = n // groups
        group = lax.rem(n, groups)
        members = pl.ds(group * GROUP, GROUP)
        own = part.at[v, x, members]
        loop(
            1,
            nx,
            lambda d: remote(own, own, xs_sem.at[v, group, d], xr_sem.at[v, group, x], {"row_1": x}).wait_send(),
        )

    loop(0, 2 * groups, sent_sums)

    def sent_mid(n):
        v = n // nz
        d = lax.rem(n, nz)

        @pl.when(d > 0)
        def _():
            to = plus_z(d)
            remote(mid.at[v, to], mid.at[v, to], zs_sem.at[v, to], zr_sem.at[v, z], {"row_0": z}).wait_send()

    loop(0, 2 * nz, sent_mid)

    def sent_group(group):
        members = all_z.at[pl.ds(group * GROUP, GROUP)]
        loop(
            1,
            nx,
            lambda d: remote(members, members, gxs_sem.at[group, d], gxr_sem.at[group, x], {"row_1": x}).wait_send(),
        )

    loop(0, groups, sent_group)
    core_copy(core_own.at[0], core_par.at[0], 2).wait_send()
    sq_core.wait_send()
    core_copy(core_own.at[1], core_par.at[1], 3).wait()
    ritz_ref[...] = core_own[1] + core_par[1]


def finish(window_total, small_in, ritz_in, metric_in, nb_ref, nd_ref, nc_ref, ritz_ref, metric_ref):
    ritz_ref[...] = ritz_in[...]
    metric_ref[...] = metric_in[...]
    nb_ref[...] = small_in[0:2, :]
    nd_ref[...] = small_in[2:4, :]
    nc_ref[...] = small_in[4:6, :] * lax.rsqrt(small_in[6:7, :] / window_total + 1e-06)


def on_device(hamiltonian_rows, current_block, correction_block, previous_block, ritz_values, mixing_coeffs):
    nz, nx = lax.axis_size("row_0"), lax.axis_size("row_1")
    groups = nz // GROUP
    owners, _, out_rows, columns = hamiltonian_rows.shape
    block_width = current_block.shape[1]
    window_total = out_rows * owners * lax.axis_size("col")
    tiles = columns // LANES
    h_flat = hamiltonian_rows.reshape(owners, out_rows, tiles, LANES).transpose(0, 2, 1, 3)
    h_flat = h_flat.reshape(owners * tiles * out_rows, LANES)
    f32 = functools.partial(jax.ShapeDtypeStruct, dtype=jnp.float32)
    vmem = pl.BlockSpec(memory_space=pltpu.VMEM)
    hbm = pl.BlockSpec(memory_space=pltpu.HBM)
    square = (block_width, block_width)

    def buffer(*shape):
        return pltpu.VMEM(shape, jnp.float32)

    sems = pltpu.SemaphoreType.DMA
    sem_shapes = (
        [(8,)]
        + [(2, groups, nx)] * 2
        + [(2, nz)] * 2
        + [(nz,)] * 2
        + [(groups, nx)] * 2
        + [(nz,)] * 2
        + [(nx,)] * 2
        + [(nz,)] * 2
        + [(nx,)] * 2
        + [(5,)] * 2
    )
    chunk = (4, LANES)
    small, ritz, metric = pl.pallas_call(
        functools.partial(kernel, nz, nx),
        out_shape=(f32((8, block_width)), f32(square), f32(square)),
        in_specs=[hbm] * 6,
        out_specs=(vmem,) * 3,
        scratch_shapes=[
            buffer(1, block_width),
            buffer(*h_flat.shape),
            buffer(3, *square),
            buffer(6, *square),
            buffer(2, 2 * owners, block_width),
            buffer(2, 2 * owners, block_width),
            buffer(2, nx, nz, *chunk),
            buffer(2, nx, nz, *chunk),
            buffer(2, nz, *chunk),
            buffer(2, nz, *chunk),
            buffer(2, *chunk),
            buffer(nz, *chunk),
            buffer(2, nx, nz, *chunk),
            buffer(*chunk),
            buffer(nz, *chunk),
            buffer(block_width, 2 * owners),
            buffer(2, LANES),
            buffer(nz, 2, LANES),
            buffer(2, LANES),
            buffer(nx, 2, LANES),
            buffer(2, *square),
            buffer(2, *square),
            buffer(2, LANES),
            buffer(2, LANES),
        ]
        + [sems(shape) for shape in sem_shapes],
        compiler_params=pltpu.CompilerParams(
            collective_id=0, has_side_effects=True, vmem_limit_bytes=MAIN_VMEM
        ),
        name="lobpcg_step",
    )(
        *(
            pltpu.with_memory_space_constraint(a, pltpu.HBM)
            for a in (
                h_flat,
                current_block,
                correction_block,
                previous_block,
                mixing_coeffs,
                ritz_values.reshape(1, -1),
            )
        )
    )
    return pl.pallas_call(
        functools.partial(finish, window_total),
        out_shape=(f32((out_rows, block_width)),) * 3 + (f32(square),) * 2,
        in_specs=[vmem] * 3,
        out_specs=(vmem,) * 5,
        compiler_params=pltpu.CompilerParams(vmem_limit_bytes=END_VMEM),
        name="finish",
    )(small, ritz, metric)


def solution(mesh):
    finer = Mesh(
        mesh.devices.reshape(mesh.shape["chan"], NZ, NX, mesh.shape["col"]),
        ("chan", "row_0", "row_1", "col"),
    )
    in_specs = (
        P("chan", "col", None, ROW),
        P(CHAN_ROW_COL, None),
        P(CHAN_ROW_COL, None),
        P(CHAN_ROW_COL, None),
        P("chan"),
        P("chan", None),
    )
    out_specs = (
        P(CHAN_ROW_COL, None),
        P(CHAN_ROW_COL, None),
        P(CHAN_ROW_COL, None),
        P("chan", None),
        P("chan", None),
    )
    return jax.shard_map(on_device, mesh=finer, in_specs=in_specs, out_specs=out_specs, check_vma=False)
```

time: 89.2 us -> 90.7 us (1.017)
  Pallas kernels: 88.4 us -> 89.9 us
    pallas_call x1, Pallas kernels: 87.6 us -> 89.1 us  [on_device(): pl.pallas_call(functools.partial(kernel, nz, nx), out_shape=(f32((8, bloc...]
where the time goes in v4:
time: 90.7 us; the launch traced here: 90.6 us
  Pallas kernels  89.9 us (99%)
    pallas_call x1, Pallas kernels, on_device(): pl.pallas_call(functools.partial(kernel, nz, nx), out_shape=(f32((8, bloc...  89.1 us

profile of v4, /device:TPU:65, one launch (start us, length us, event | category | flops | bytes accessed | tf_op | source)
XLA Modules:
  0.0 90.6 jit_solution(4019437156869578379)
XLA Ops:
  0.6 89.1 %lobpcg_step.1 = (f32[8,256]{1,0:T(8,128)S(1)}, f32[256,256]{1,0:T(8,128)S(1)}, f32[256,256]{1,0:T(8,128)S(1)}) custom-call(f32[1024,128]{1,0:T(8,128)} %bitcast.6, f32[256,256]{1,0:T(8,128)} %x_hbm.1, f32[256,256]{1,0:T(8,128)} %w_hbm.1, f32[256,256]{1,0:T(8,128)} %p_hbm.1, f32[768,256]{1,0:T(8,128)} %c_hbm.1, f32[1,256]{1,0:T(1,128)} %bitcast.7), custom_call_target="tpu_custom_call" | custom-call | tf_op jit(solution)/shard_map/lobpcg_step/pallas_call | solution.py:470
  89.7 0.8 finish.1

commit v5 on v4

--- a/solution.py
+++ b/solution.py
@@ -67,8 +67,6 @@
     sq_all_x,
     core_own,
     core_par,
-    sq_own,
-    sq_par,
     in_sem,
     xs_sem,
     xr_sem,
@@ -123,23 +121,32 @@
 
         lax.fori_loop(first, last, step, 0)
 
+    def far(i, n):
+        return n // 2 + (i + 1) // 2 * (1 - 2 * lax.rem(i, 2))
+
+    def each_z(body):
+        loop(0, nz - 1, lambda i: body(far(i, nz)))
+
+    def each_x(body):
+        loop(0, nx - 1, lambda i: body(far(i, nx)))
+
     def send_all_z(src, into, s_sem, r_sem):
-        loop(1, nz, lambda d: remote(src, into.at[z], s_sem.at[d], r_sem.at[z], {"row_0": plus_z(d)}).start())
+        each_z(lambda d: remote(src, into.at[z], s_sem.at[d], r_sem.at[z], {"row_0": plus_z(d)}).start())
 
     def got_all_z(into, s_sem, r_sem):
-        loop(1, nz, lambda d: remote(into.at[z], into.at[z], s_sem.at[d], r_sem.at[plus_z(d)], {"row_0": z}).wait_recv())
+        each_z(lambda d: remote(into.at[z], into.at[z], s_sem.at[d], r_sem.at[plus_z(d)], {"row_0": z}).wait_recv())
 
     def sent_all_z(src, s_sem, r_sem):
-        loop(1, nz, lambda d: remote(src, src, s_sem.at[d], r_sem.at[z], {"row_0": z}).wait_send())
+        each_z(lambda d: remote(src, src, s_sem.at[d], r_sem.at[z], {"row_0": z}).wait_send())
 
     def send_all_x(src, into, s_sem, r_sem):
-        loop(1, nx, lambda d: remote(src, into.at[x], s_sem.at[d], r_sem.at[x], {"row_1": plus_x(d)}).start())
+        each_x(lambda d: remote(src, into.at[x], s_sem.at[d], r_sem.at[x], {"row_1": plus_x(d)}).start())
 
     def got_all_x(into, s_sem, r_sem):
-        loop(1, nx, lambda d: remote(into.at[x], into.at[x], s_sem.at[d], r_sem.at[plus_x(d)], {"row_1": x}).wait_recv())
+        each_x(lambda d: remote(into.at[x], into.at[x], s_sem.at[d], r_sem.at[plus_x(d)], {"row_1": x}).wait_recv())
 
     def sent_all_x(src, s_sem, r_sem):
-        loop(1, nx, lambda d: remote(src, src, s_sem.at[d], r_sem.at[x], {"row_1": x}).wait_send())
+        each_x(lambda d: remote(src, src, s_sem.at[d], r_sem.at[x], {"row_1": x}).wait_send())
 
     def core_copy(src, dst, i):
         return remote(src, dst, cs_sem.at[i], cr_sem.at[i], {"col": other})
@@ -161,9 +168,17 @@
         loads[i].start()
 
     barrier = pltpu.get_barrier_semaphore()
-    loop(1, nz, lambda d: pl.semaphore_signal(barrier, inc=1, device_id={"row_0": plus_z(d)}, device_id_type=MESH))
-    loop(1, nx, lambda d: pl.semaphore_signal(barrier, inc=1, device_id={"row_1": plus_x(d)}, device_id_type=MESH))
-    pl.semaphore_signal(barrier, inc=1, device_id={"col": other}, device_id_type=MESH)
+    def signal(device):
+        pl.semaphore_signal(barrier, inc=1, device_id=device, device_id_type=MESH)
+
+    def both_cores(body):
+        loop(1, 2 * nx, lambda n: body(n // nx, lax.rem(n, nx)))
+
+    def core_of(which):
+        return core + which * (1 - 2 * core)
+
+    each_z(lambda d: signal({"row_0": plus_z(d)}))
+    both_cores(lambda which, d: signal({"row_1": plus_x(d), "col": core_of(which)}))
 
     for load in loads[:6]:
         load.wait()
@@ -180,7 +195,7 @@
         for q in range(2):
             nb_tile[j * 2 + q : j * 2 + q + 1, :] = rows[4, j : j + 1, q * LANES : (q + 1) * LANES]
 
-    pl.semaphore_wait(barrier, nz + nx - 1)
+    pl.semaphore_wait(barrier, nz - 1 + 2 * nx - 1)
     y_core = core_copy(rows.at[4], rows.at[5], 1)
     y_core.start()
     x_core = core_copy(rows.at[2], rows.at[3], 0)
@@ -218,77 +233,79 @@
                 block = value[j * owners : (j + 1) * owners, q * LANES : (q + 1) * LANES]
                 part[v, :, :, j * 2 + q, :] = block.reshape(nx, nz, LANES)
 
-        def send_group(k):
-            group = far_group(k)
-            members = pl.ds(group * GROUP, GROUP)
-            loop(
-                1,
-                nx,
-                lambda d: remote(
-                    part.at[v, plus_x(d), members],
-                    in_x.at[v, x, members],
-                    xs_sem.at[v, group, d],
-                    xr_sem.at[v, group, x],
-                    {"row_1": plus_x(d)},
-                ).start(),
-            )
-
-        loop(0, groups, send_group)
+        each_x(
+            lambda d: remote(
+                part.at[v, plus_x(d)], in_x.at[v, x], xs_sem.at[v, d], xr_sem.at[v, x], {"row_1": plus_x(d)}
+            ).start()
+        )
 
     loop(0, 2, other_product)
 
-    def pass_group(n):
-        v = n // groups
-        k = lax.rem(n, groups)
+    def sum_x(v):
+        own = part.at[v, x]
+        each_x(
+            lambda d: remote(own, in_x.at[v, x], xs_sem.at[v, d], xr_sem.at[v, plus_x(d)], {"row_1": x}).wait_recv()
+        )
+        total = part[v, x]
+        for d in range(1, nx):
+            total = total + in_x[v, plus_x(d)]
+        mid[v] = total
+        each_z(
+            lambda d: remote(
+                mid.at[v, plus_z(d)], in_z.at[v, z], zs_sem.at[v, d], zr_sem.at[v, z], {"row_0": plus_z(d)}
+            ).start()
+        )
+
+    def sum_z(v):
+        each_z(
+            lambda d: remote(
+                mid.at[v, z], in_z.at[v, z], zs_sem.at[v, d], zr_sem.at[v, plus_z(d)], {"row_0": z}
+            ).wait_recv()
+        )
+        total = mid[v, z]
+        for d in range(1, nz):
+            total = total + in_z[v, plus_z(d)]
+        tile[v] = total
+
+    sum_x(0)
+
+    sum_z(0)
+    send_all_z(tile.at[0], all_z, gzs_sem, gzr_sem)
+    all_z[z] = tile[0]
+
+    def forward(n):
+        k = groups - 1 - n
         group = far_group(k)
         members = pl.ds(group * GROUP, GROUP)
-        own = part.at[v, x, members]
+
+        def got_member(m):
+            s = member(group, m)
+            remote(all_z.at[s], all_z.at[s], gzs_sem.at[0], gzr_sem.at[s], {"row_0": z}).wait_recv()
+
+        @pl.when(k < groups - 1)
+        def _():
+            got_member(0)
+
+        loop(1, GROUP, got_member)
         loop(
             1,
             nx,
             lambda d: remote(
-                own, in_x.at[v, x, members], xs_sem.at[v, group, d], xr_sem.at[v, group, plus_x(d)], {"row_1": x}
-            ).wait_recv(),
-        )
-        total = part[v, x, members]
-        for d in range(1, nx):
-            total = total + in_x[v, plus_x(d), members]
-        mid[v, members] = total
-
-        def send_member(m):
-            to = member(group, m)
-            remote(mid.at[v, to], in_z.at[v, z], zs_sem.at[v, to], zr_sem.at[v, z], {"row_0": to}).start()
-
-        @pl.when(k < groups - 1)
-        def _():
-            send_member(0)
-
-        loop(1, GROUP, send_member)
-
-    loop(0, 2 * groups, pass_group)
-
-    def sum_z(v):
-        loop(
-            1,
-            nz,
-            lambda d: remote(
-                mid.at[v, z], in_z.at[v, z], zs_sem.at[v, z], zr_sem.at[v, plus_z(d)], {"row_0": z}
-            ).wait_recv(),
-        )
-        total = mid[v, z]
-        for d in range(1, nz):
-            total = total + in_z[v, plus_z(d)]
-        tile[v] = total
-
-    sum_z(0)
-    send_all_z(tile.at[0], all_z, gzs_sem, gzr_sem)
-    all_z[z] = tile[0]
+                all_z.at[members],
+                gathered.at[1, x, members],
+                gxs_sem.at[group, d],
+                gxr_sem.at[group, x],
+                {"row_1": plus_x(d)},
+            ).start(),
+        )
 
     got_all_z(nb_all_z, nzs_sem, nzr_sem)
     nb_all_z[z] = nb_tile[...]
     send_all_x(nb_all_z, gathered.at[0], nxs_sem, nxr_sem)
     gathered[0, x] = nb_all_z[...]
 
+    sum_x(1)
+    forward(0)
     sum_z(1)
     for q in range(2):
         squares = 0.0
@@ -301,33 +318,7 @@
     send_all_z(sq_tile, sq_all_z, qzs_sem, qzr_sem)
     sq_all_z[z] = sq_tile[...]
 
-    def forward(n):
-        k = groups - 1 - n
-        group = far_group(k)
-        members = pl.ds(group * GROUP, GROUP)
-
-        def got_member(m):
-            s = member(group, m)
-            remote(all_z.at[s], all_z.at[s], gzs_sem.at[0], gzr_sem.at[s], {"row_0": z}).wait_recv()
-
-        @pl.when(k < groups - 1)
-        def _():
-            got_member(0)
-
-        loop(1, GROUP, got_member)
-        loop(
-            1,
-            nx,
-            lambda d: remote(
-                all_z.at[members],
-                gathered.at[1, x, members],
-                gxs_sem.at[group, d],
-                gxr_sem.at[group, x],
-                {"row_1": plus_x(d)},
-            ).start(),
-        )
-
-    loop(0, groups, forward)
+    loop(1, groups, forward)
     gathered[1, x] = all_z[...]
 
     def rows_of(u):
@@ -344,11 +335,6 @@
     def last_product(u):
         @pl.when(u == 1)
         def _():
-            got_all_z(sq_all_z, qzs_sem, qzr_sem)
-            sq_sum[...] = jnp.sum(sq_all_z[...], axis=0)
-            send_all_x(sq_sum, sq_all_x, qxs_sem, qxr_sem)
-            sq_all_x[x] = sq_sum[...]
-
             def got_group(group):
                 members = pl.ds(group * GROUP, GROUP)
                 loop(
@@ -370,16 +356,21 @@
 
     loop(0, 2, last_product)
 
-    got_all_x(sq_all_x, qxs_sem, qxr_sem)
-    sq_own[...] = jnp.sum(sq_all_x[...], axis=0)
-    sq_core = core_copy(sq_own, sq_par, 4)
-    sq_core.start()
+    got_all_z(sq_all_z, qzs_sem, qzr_sem)
+    sq_sum[...] = jnp.sum(sq_all_z[...], axis=0)
+    both_cores(
+        lambda which, d: remote(
+            sq_sum,
+            sq_all_x.at[core, x],
+            qxs_sem.at[which, d],
+            qxr_sem.at[core, x],
+            {"row_1": plus_x(d), "col": core_of(which)},
+        ).start()
+    )
+    sq_all_x[core, x] = sq_sum[...]
     core_copy(core_own.at[0], core_par.at[0], 2).wait_recv()
     metric_ref[...] = core_own[0] + core_par[0]
     small_ref[7:8, :] = jnp.zeros((1, small_ref.shape[1]), jnp.float32)
-    sq_core.wait_recv()
-    for q in range(2):
-        small_ref[6:7, q * LANES : (q + 1) * LANES] = sq_own[q : q + 1, :] + sq_par[q : q + 1, :]
 
     y_core.wait_send()
     x_core.wait_send()
@@ -387,31 +378,16 @@
     sent_all_z(tile.at[0], gzs_sem, gzr_sem)
     sent_all_z(sq_tile, qzs_sem, qzr_sem)
     sent_all_x(nb_all_z, nxs_sem, nxr_sem)
-    sent_all_x(sq_sum, qxs_sem, qxr_sem)
-
-    def sent_sums(n):
-        v = n // groups
-        group = lax.rem(n, groups)
-        members = pl.ds(group * GROUP, GROUP)
-        own = part.at[v, x, members]
-        loop(
-            1,
-            nx,
-            lambda d: remote(own, own, xs_sem.at[v, group, d], xr_sem.at[v, group, x], {"row_1": x}).wait_send(),
-        )
-
-    loop(0, 2 * groups, sent_sums)
-
-    def sent_mid(n):
-        v = n // nz
-        d = lax.rem(n, nz)
-
-        @pl.when(d > 0)
-        def _():
-            to = plus_z(d)
-            remote(mid.at[v, to], mid.at[v, to], zs_sem.at[v, to], zr_sem.at[v, z], {"row_0": z}).wait_send()
-
-    loop(0, 2 * nz, sent_mid)
+
+    def sent_sums(v):
+        each_x(
+            lambda d: remote(part.at[v, x], part.at[v, x], xs_sem.at[v, d], xr_sem.at[v, x], {"row_1": x}).wait_send()
+        )
+        each_z(
+            lambda d: remote(mid.at[v, z], mid.at[v, z], zs_sem.at[v, d], zr_sem.at[v, z], {"row_0": z}).wait_send()
+        )
+
+    loop(0, 2, sent_sums)
 
     def sent_group(group):
         members = all_z.at[pl.ds(group * GROUP, GROUP)]
@@ -423,9 +399,20 @@
 
     loop(0, groups, sent_group)
     core_copy(core_own.at[0], core_par.at[0], 2).wait_send()
-    sq_core.wait_send()
     core_copy(core_own.at[1], core_par.at[1], 3).wait()
     ritz_ref[...] = core_own[1] + core_par[1]
+    both_cores(
+        lambda which, d: remote(
+            sq_sum,
+            sq_all_x.at[core, x],
+            qxs_sem.at[which, d],
+            qxr_sem.at[core_of(which), plus_x(d)],
+            {"row_1": x, "col": other},
+        ).wait()
+    )
+    squares = jnp.sum(jnp.sum(sq_all_x[...], axis=0), axis=0)
+    for q in range(2):
+        small_ref[6:7, q * LANES : (q + 1) * LANES] = squares[q : q + 1, :]
 
 
 def finish(window_total, small_in, ritz_in, metric_in, nb_ref, nd_ref, nc_ref, ritz_ref, metric_ref):
@@ -456,15 +443,15 @@
     sems = pltpu.SemaphoreType.DMA
     sem_shapes = (
         [(8,)]
-        + [(2, groups, nx)] * 2
+        + [(2, nx)] * 2
         + [(2, nz)] * 2
         + [(nz,)] * 2
         + [(groups, nx)] * 2
         + [(nz,)] * 2
-        + [(nx,)] * 2
+        + [(2, nx)] * 2
         + [(nz,)] * 2
         + [(nx,)] * 2
-        + [(5,)] * 2
+        + [(4,)] * 2
     )
     chunk = (4, LANES)
     small, ritz, metric = pl.pallas_call(
@@ -492,11 +479,9 @@
             buffer(2, LANES),
             buffer(nz, 2, LANES),
             buffer(2, LANES),
-            buffer(nx, 2, LANES),
+            buffer(2, nx, 2, LANES),
             buffer(2, *square),
             buffer(2, *square),
-            buffer(2, LANES),
-            buffer(2, LANES),
         ]
         + [sems(shape) for shape in sem_shapes],
         compiler_params=pltpu.CompilerParams(

time: 90.7 us -> 91.6 us (level)
  no operation moved by 1% of the time
where the time goes in v5:
time: 91.6 us; the launch traced here: 91.5 us
  Pallas kernels  90.8 us (99%)
    pallas_call x1, Pallas kernels, on_device(): pl.pallas_call(functools.partial(kernel, nz, nx), out_shape=(f32((8, bloc...  90 us

profile of v5, /device:TPU:65, one launch (start us, length us, event | category | flops | bytes accessed | tf_op | source)
XLA Modules:
  0.0 91.5 jit_solution(7163744624286998340)
XLA Ops:
  0.6 90.0 %lobpcg_step.1 = (f32[8,256]{1,0:T(8,128)S(1)}, f32[256,256]{1,0:T(8,128)S(1)}, f32[256,256]{1,0:T(8,128)S(1)}) custom-call(f32[1024,128]{1,0:T(8,128)} %bitcast.6, f32[256,256]{1,0:T(8,128)} %x_hbm.1, f32[256,256]{1,0:T(8,128)} %w_hbm.1, f32[256,256]{1,0:T(8,128)} %p_hbm.1, f32[768,256]{1,0:T(8,128)} %c_hbm.1, f32[1,256]{1,0:T(1,128)} %bitcast.7), custom_call_target="tpu_custom_call" | custom-call | tf_op jit(solution)/shard_map/lobpcg_step/pallas_call | solution.py:457
  90.6 0.8 finish.1

commit v6 on v5

--- a/solution.py
+++ b/solution.py
@@ -51,10 +51,14 @@
     rows,
     h_rows,
     prod,
-    part,
-    in_x,
-    mid,
-    in_z,
+    y_part,
+    y_in,
+    y_mid,
+    y_mid_in,
+    x_part,
+    x_in,
+    x_mid,
+    x_mid_in,
     tile,
     all_z,
     gathered,
@@ -68,10 +72,14 @@
     core_own,
     core_par,
     in_sem,
-    xs_sem,
-    xr_sem,
-    zs_sem,
-    zr_sem,
+    yxs_sem,
+    yxr_sem,
+    yzs_sem,
+    yzr_sem,
+    xzs_sem,
+    xzr_sem,
+    xxs_sem,
+    xxr_sem,
     gzs_sem,
     gzr_sem,
     gxs_sem,
@@ -148,6 +156,30 @@
     def sent_all_x(src, s_sem, r_sem):
         each_x(lambda d: remote(src, src, s_sem.at[d], r_sem.at[x], {"row_1": x}).wait_send())
 
+    def scatter_z(parts, into, s_sem, r_sem):
+        each_z(
+            lambda d: remote(
+                parts.at[plus_z(d)], into.at[z], s_sem.at[d], r_sem.at[z], {"row_0": plus_z(d)}
+            ).start()
+        )
+
+    def scatter_x(parts, into, s_sem, r_sem):
+        each_x(
+            lambda d: remote(
+                parts.at[plus_x(d)], into.at[x], s_sem.at[d], r_sem.at[x], {"row_1": plus_x(d)}
+            ).start()
+        )
+
+    def total_z(own, into):
+        for d in range(1, nz):
+            own = own + into[plus_z(d)]
+        return own
+
+    def total_x(own, into):
+        for d in range(1, nx):
+            own = own + into[plus_x(d)]
+        return own
+
     def core_copy(src, dst, i):
         return remote(src, dst, cs_sem.at[i], cr_sem.at[i], {"col": other})
 
@@ -195,13 +227,6 @@
         for q in range(2):
             nb_tile[j * 2 + q : j * 2 + q + 1, :] = rows[4, j : j + 1, q * LANES : (q + 1) * LANES]
 
-    pl.semaphore_wait(barrier, nz - 1 + 2 * nx - 1)
-    y_core = core_copy(rows.at[4], rows.at[5], 1)
-    y_core.start()
-    x_core = core_copy(rows.at[2], rows.at[3], 0)
-    x_core.start()
-    send_all_z(nb_tile, nb_all_z, nzs_sem, nzr_sem)
-
     loads[6].wait()
     loads[7].wait()
     tiles = half // LANES
@@ -223,55 +248,75 @@
         prod[v] = dot(h_rows[0], rows[4 - 2 * v])
 
     loop(0, 2, own_product)
-    y_core.wait_recv()
-    x_core.wait_recv()
+    pl.semaphore_wait(barrier, nz - 1 + 2 * nx - 1)
+    y_core = core_copy(rows.at[4], rows.at[5], 1)
+    y_core.start()
+    x_core = core_copy(rows.at[2], rows.at[3], 0)
+    x_core.start()
+    send_all_z(nb_tile, nb_all_z, nzs_sem, nzr_sem)
 
     def other_product(v):
-        value = prod[v] + dot(h_rows[1], rows[5 - 2 * v])
-        for j in range(2):
-            for q in range(2):
-                block = value[j * owners : (j + 1) * owners, q * LANES : (q + 1) * LANES]
-                part[v, :, :, j * 2 + q, :] = block.reshape(nx, nz, LANES)
-
-        each_x(
-            lambda d: remote(
-                part.at[v, plus_x(d)], in_x.at[v, x], xs_sem.at[v, d], xr_sem.at[v, x], {"row_1": plus_x(d)}
-            ).start()
-        )
+        @pl.when(v == 0)
+        def _():
+            y_core.wait_recv()
+
+        @pl.when(v == 1)
+        def _():
+            x_core.wait_recv()
+
+        prod[v] += dot(h_rows[1], rows[5 - 2 * v])
+
+        def blocks():
+            for j in range(2):
+                for q in range(2):
+                    block = prod[v, j * owners : (j + 1) * owners, q * LANES : (q + 1) * LANES]
+                    yield j * 2 + q, block.reshape(nx, nz, LANES)
+
+        @pl.when(v == 0)
+        def _():
+            for row, block in blocks():
+                y_part[:, :, row, :] = block
+            scatter_x(y_part, y_in, yxs_sem, yxr_sem)
+
+        @pl.when(v == 1)
+        def _():
+            for row, block in blocks():
+                for owner_x in range(nx):
+                    x_part[:, owner_x, row, :] = block[owner_x]
+            scatter_z(x_part, x_in, xzs_sem, xzr_sem)
 
     loop(0, 2, other_product)
 
-    def sum_x(v):
-        own = part.at[v, x]
-        each_x(
-            lambda d: remote(own, in_x.at[v, x], xs_sem.at[v, d], xr_sem.at[v, plus_x(d)], {"row_1": x}).wait_recv()
-        )
-        total = part[v, x]
-        for d in range(1, nx):
-            total = total + in_x[v, plus_x(d)]
-        mid[v] = total
-        each_z(
-            lambda d: remote(
-                mid.at[v, plus_z(d)], in_z.at[v, z], zs_sem.at[v, d], zr_sem.at[v, z], {"row_0": plus_z(d)}
-            ).start()
-        )
-
-    def sum_z(v):
-        each_z(
-            lambda d: remote(
-                mid.at[v, z], in_z.at[v, z], zs_sem.at[v, d], zr_sem.at[v, plus_z(d)], {"row_0": z}
-            ).wait_recv()
-        )
-        total = mid[v, z]
-        for d in range(1, nz):
-            total = total + in_z[v, plus_z(d)]
-        tile[v] = total
-
-    sum_x(0)
-
-    sum_z(0)
+    got_all_x(y_in, yxs_sem, yxr_sem)
+    y_mid[...] = total_x(y_part[x], y_in)
+    scatter_z(y_mid, y_mid_in, yzs_sem, yzr_sem)
+
+    got_all_z(nb_all_z, nzs_sem, nzr_sem)
+    nb_all_z[z] = nb_tile[...]
+    send_all_x(nb_all_z, gathered.at[0], nxs_sem, nxr_sem)
+    gathered[0, x] = nb_all_z[...]
+
+    got_all_z(x_in, xzs_sem, xzr_sem)
+    x_mid[...] = total_z(x_part[z], x_in)
+    scatter_x(x_mid, x_mid_in, xxs_sem, xxr_sem)
+
+    got_all_z(y_mid_in, yzs_sem, yzr_sem)
+    tile[0] = total_z(y_mid[z], y_mid_in)
     send_all_z(tile.at[0], all_z, gzs_sem, gzr_sem)
     all_z[z] = tile[0]
+
+    got_all_x(x_mid_in, xxs_sem, xxr_sem)
+    tile[1] = total_x(x_mid[x], x_mid_in)
+    for q in range(2):
+        squares = 0.0
+        for j in range(2):
+            columns = slice(q * LANES, (q + 1) * LANES)
+            residual = tile[1, j * 2 + q : j * 2 + q + 1, :] - rows[2, j : j + 1, columns] * rv_ref[:, columns]
+            small_ref[4 + j : 5 + j, columns] = residual
+            squares = squares + residual * residual
+        sq_tile[q : q + 1, :] = squares
+    send_all_z(sq_tile, sq_all_z, qzs_sem, qzr_sem)
+    sq_all_z[z] = sq_tile[...]
 
     def forward(n):
         k = groups - 1 - n
@@ -299,26 +344,7 @@
             ).start(),
         )
 
-    got_all_z(nb_all_z, nzs_sem, nzr_sem)
-    nb_all_z[z] = nb_tile[...]
-    send_all_x(nb_all_z, gathered.at[0], nxs_sem, nxr_sem)
-    gathered[0, x] = nb_all_z[...]
-
-    sum_x(1)
-    forward(0)
-    sum_z(1)
-    for q in range(2):
-        squares = 0.0
-        for j in range(2):
-            columns = slice(q * LANES, (q + 1) * LANES)
-            residual = tile[1, j * 2 + q : j * 2 + q + 1, :] - rows[2, j : j + 1, columns] * rv_ref[:, columns]
-            small_ref[4 + j : 5 + j, columns] = residual
-            squares = squares + residual * residual
-        sq_tile[q : q + 1, :] = squares
-    send_all_z(sq_tile, sq_all_z, qzs_sem, qzr_sem)
-    sq_all_z[z] = sq_tile[...]
-
-    loop(1, groups, forward)
+    loop(0, groups, forward)
     gathered[1, x] = all_z[...]
 
     def rows_of(u):
@@ -335,18 +361,29 @@
     def last_product(u):
         @pl.when(u == 1)
         def _():
+            got_all_z(sq_all_z, qzs_sem, qzr_sem)
+            sq_sum[...] = jnp.sum(sq_all_z[...], axis=0)
+            both_cores(
+                lambda which, d: remote(
+                    sq_sum,
+                    sq_all_x.at[core, x],
+                    qxs_sem.at[which, d],
+                    qxr_sem.at[core, x],
+                    {"row_1": plus_x(d), "col": core_of(which)},
+                ).start()
+            )
+            sq_all_x[core, x] = sq_sum[...]
+
             def got_group(group):
                 members = pl.ds(group * GROUP, GROUP)
-                loop(
-                    1,
-                    nx,
+                each_x(
                     lambda d: remote(
                         all_z.at[members],
                         gathered.at[1, x, members],
                         gxs_sem.at[group, d],
                         gxr_sem.at[group, plus_x(d)],
                         {"row_1": x},
-                    ).wait_recv(),
+                    ).wait_recv()
                 )
 
             loop(0, groups, got_group)
@@ -354,51 +391,36 @@
         core_own[u] = dot(nb_t[...], rows_of(u))
         remote(core_own.at[u], core_par.at[u], cs_sem.at[2 + u], cr_sem.at[2 + u], {"col": other}).start()
 
+        @pl.when(u == 0)
+        def _():
+            y_core.wait_send()
+            x_core.wait_send()
+            sent_all_z(nb_tile, nzs_sem, nzr_sem)
+            sent_all_x(y_part.at[x], yxs_sem, yxr_sem)
+            sent_all_z(y_mid.at[z], yzs_sem, yzr_sem)
+            sent_all_z(x_part.at[z], xzs_sem, xzr_sem)
+            sent_all_x(x_mid.at[x], xxs_sem, xxr_sem)
+            sent_all_x(nb_all_z, nxs_sem, nxr_sem)
+            sent_all_z(tile.at[0], gzs_sem, gzr_sem)
+
+        @pl.when(u == 1)
+        def _():
+            core_copy(core_own.at[0], core_par.at[0], 2).wait()
+            metric_ref[...] = core_own[0] + core_par[0]
+            sent_all_z(sq_tile, qzs_sem, qzr_sem)
+
+            def sent_group(group):
+                members = all_z.at[pl.ds(group * GROUP, GROUP)]
+                each_x(
+                    lambda d: remote(
+                        members, members, gxs_sem.at[group, d], gxr_sem.at[group, x], {"row_1": x}
+                    ).wait_send()
+                )
+
+            loop(0, groups, sent_group)
+
+    small_ref[7:8, :] = jnp.zeros((1, small_ref.shape[1]), jnp.float32)
     loop(0, 2, last_product)
-
-    got_all_z(sq_all_z, qzs_sem, qzr_sem)
-    sq_sum[...] = jnp.sum(sq_all_z[...], axis=0)
-    both_cores(
-        lambda which, d: remote(
-            sq_sum,
-            sq_all_x.at[core, x],
-            qxs_sem.at[which, d],
-            qxr_sem.at[core, x],
-            {"row_1": plus_x(d), "col": core_of(which)},
-        ).start()
-    )
-    sq_all_x[core, x] = sq_sum[...]
-    core_copy(core_own.at[0], core_par.at[0], 2).wait_recv()
-    metric_ref[...] = core_own[0] + core_par[0]
-    small_ref[7:8, :] = jnp.zeros((1, small_ref.shape[1]), jnp.float32)
-
-    y_core.wait_send()
-    x_core.wait_send()
-    sent_all_z(nb_tile, nzs_sem, nzr_sem)
-    sent_all_z(tile.at[0], gzs_sem, gzr_sem)
-    sent_all_z(sq_tile, qzs_sem, qzr_sem)
-    sent_all_x(nb_all_z, nxs_sem, nxr_sem)
-
-    def sent_sums(v):
-        each_x(
-            lambda d: remote(part.at[v, x], part.at[v, x], xs_sem.at[v, d], xr_sem.at[v, x], {"row_1": x}).wait_send()
-        )
-        each_z(
-            lambda d: remote(mid.at[v, z], mid.at[v, z], zs_sem.at[v, d], zr_sem.at[v, z], {"row_0": z}).wait_send()
-        )
-
-    loop(0, 2, sent_sums)
-
-    def sent_group(group):
-        members = all_z.at[pl.ds(group * GROUP, GROUP)]
-        loop(
-            1,
-            nx,
-            lambda d: remote(members, members, gxs_sem.at[group, d], gxr_sem.at[group, x], {"row_1": x}).wait_send(),
-        )
-
-    loop(0, groups, sent_group)
-    core_copy(core_own.at[0], core_par.at[0], 2).wait_send()
     core_copy(core_own.at[1], core_par.at[1], 3).wait()
     ritz_ref[...] = core_own[1] + core_par[1]
     both_cores(
@@ -443,8 +465,9 @@
     sems = pltpu.SemaphoreType.DMA
     sem_shapes = (
         [(8,)]
-        + [(2, nx)] * 2
-        + [(2, nz)] * 2
+        + [(nx,)] * 2
+        + [(nz,)] * 4
+        + [(nx,)] * 2
         + [(nz,)] * 2
         + [(groups, nx)] * 2
         + [(nz,)] * 2
@@ -466,10 +489,14 @@
             buffer(6, *square),
             buffer(2, 2 * owners, block_width),
             buffer(2, 2 * owners, block_width),
-            buffer(2, nx, nz, *chunk),
-            buffer(2, nx, nz, *chunk),
-            buffer(2, nz, *chunk),
-            buffer(2, nz, *chunk),
+            buffer(nx, nz, *chunk),
+            buffer(nx, nz, *chunk),
+            buffer(nz, *chunk),
+            buffer(nz, *chunk),
+            buffer(nz, nx, *chunk),
+            buffer(nz, nx, *chunk),
+            buffer(nx, *chunk),
+            buffer(nx, *chunk),
             buffer(2, *chunk),
             buffer(nz, *chunk),
             buffer(2, nx, nz, *chunk),

time: 91.6 us -> 89.9 us (0.981)
  Pallas kernels: 90.8 us -> 89.2 us
    pallas_call x1, Pallas kernels: 90 us -> 88.3 us  [on_device(): pl.pallas_call(functools.partial(kernel, nz, nx), out_shape=(f32((8, bloc...]
where the time goes in v6:
time: 89.9 us; the launch traced here: 89.8 us
  Pallas kernels  89.2 us (99%)
    pallas_call x1, Pallas kernels, on_device(): pl.pallas_call(functools.partial(kernel, nz, nx), out_shape=(f32((8, bloc...  88.3 us

profile of v6, /device:TPU:65, one launch (start us, length us, event | category | flops | bytes accessed | tf_op | source)
XLA Modules:
  0.0 89.8 jit_solution(4716102366884397752)
XLA Ops:
  0.6 88.3 %lobpcg_step.1 = (f32[8,256]{1,0:T(8,128)S(1)}, f32[256,256]{1,0:T(8,128)S(1)}, f32[256,256]{1,0:T(8,128)S(1)}) custom-call(f32[1024,128]{1,0:T(8,128)} %bitcast.6, f32[256,256]{1,0:T(8,128)} %x_hbm.1, f32[256,256]{1,0:T(8,128)} %w_hbm.1, f32[256,256]{1,0:T(8,128)} %p_hbm.1, f32[768,256]{1,0:T(8,128)} %c_hbm.1, f32[1,256]{1,0:T(1,128)} %bitcast.7), custom_call_target="tpu_custom_call" | custom-call | tf_op jit(solution)/shard_map/lobpcg_step/pallas_call | solution.py:480
  89.0 0.8 finish.1

commit v7 on v6

--- a/solution.py
+++ b/solution.py
@@ -51,14 +51,12 @@
     rows,
     h_rows,
     prod,
-    y_part,
-    y_in,
-    y_mid,
-    y_mid_in,
-    x_part,
-    x_in,
-    x_mid,
-    x_mid_in,
+    part,
+    part_in,
+    hop_in,
+    hop,
+    mid,
+    mid_in,
     tile,
     all_z,
     gathered,
@@ -72,14 +70,14 @@
     core_own,
     core_par,
     in_sem,
-    yxs_sem,
-    yxr_sem,
-    yzs_sem,
-    yzr_sem,
-    xzs_sem,
-    xzr_sem,
-    xxs_sem,
-    xxr_sem,
+    ps_sem,
+    pr_sem,
+    fs_sem,
+    fr_sem,
+    hs_sem,
+    hr_sem,
+    zs_sem,
+    zr_sem,
     gzs_sem,
     gzr_sem,
     gxs_sem,
@@ -108,7 +106,7 @@
         return lax.rem(z + d, nz)
 
     def plus_x(d):
-        return lax.rem(x + d, nx)
+        return lax.rem(x + d + nx, nx)
 
     def far_group(k):
         step = (k + 1) // 2
@@ -156,29 +154,91 @@
     def sent_all_x(src, s_sem, r_sem):
         each_x(lambda d: remote(src, src, s_sem.at[d], r_sem.at[x], {"row_1": x}).wait_send())
 
-    def scatter_z(parts, into, s_sem, r_sem):
+    opposite = nx // 2
+    whole = [d for d in range(1 - opposite, opposite) if abs(d) not in (0, opposite - 1)]
+
+    def half_of(side):
+        return pl.ds(side * (nz // 2), nz // 2)
+
+    def hop_copy(v, side, to):
+        sign = 1 - 2 * side
+        return remote(
+            part.at[v, plus_x(opposite), half_of(side)],
+            hop_in.at[v, side],
+            hs_sem.at[v, side],
+            hr_sem.at[v, side],
+            {"row_1": plus_x(sign * to)},
+        )
+
+    def half_copy(v, side, hopped, src, source, to):
+        half_z = half_of(side if hopped else 1 - side)
+        return remote(
+            src if hopped else part.at[v, to, half_z],
+            part_in.at[v, source, half_z],
+            fs_sem.at[v, side, hopped],
+            fr_sem.at[v, side, hopped],
+            {"row_1": to},
+        )
+
+    def whole_copy(v, d, source, to):
+        return remote(
+            part.at[v, to], part_in.at[v, source], ps_sem.at[v, d % nx], pr_sem.at[v, source], {"row_1": to}
+        )
+
+    def start_sum(v):
+        for side in range(2):
+            hop_copy(v, side, 1).start()
+        for d in sorted(whole, key=lambda d: -abs(d)):
+            whole_copy(v, d, x, plus_x(d)).start()
+        for side in range(2):
+            half_copy(v, side, 0, None, x, plus_x((1 - 2 * side) * (opposite - 1))).start()
+
+    def hop_on(v):
+        for side in range(2):
+            to = plus_x((1 - 2 * side) * (opposite - 1))
+            hop_copy(v, side, 1).wait_recv()
+            hop[v, side] = hop_in[v, side] + part[v, to, half_of(side)]
+            half_copy(v, side, 1, hop.at[v, side], x, to).start()
+
+    def sum_x(v):
+        for d in whole:
+            whole_copy(v, d, plus_x(d), plus_x(d)).wait_recv()
+        for side in range(2):
+            source = plus_x(-(1 - 2 * side) * (opposite - 1))
+            for hopped in range(2):
+                half_copy(v, side, hopped, hop.at[v, side], source, source).wait_recv()
+        total = part[v, x]
+        for d in range(1 - opposite, opposite):
+            if d:
+                total = total + part_in[v, plus_x(d)]
+        mid[v] = total
         each_z(
             lambda d: remote(
-                parts.at[plus_z(d)], into.at[z], s_sem.at[d], r_sem.at[z], {"row_0": plus_z(d)}
+                mid.at[v, plus_z(d)], mid_in.at[v, z], zs_sem.at[v, d], zr_sem.at[v, z], {"row_0": plus_z(d)}
             ).start()
         )
 
-    def scatter_x(parts, into, s_sem, r_sem):
-        each_x(
+    def sum_z(v):
+        each_z(
             lambda d: remote(
-                parts.at[plus_x(d)], into.at[x], s_sem.at[d], r_sem.at[x], {"row_1": plus_x(d)}
-            ).start()
-        )
-
-    def total_z(own, into):
+                mid.at[v, z], mid_in.at[v, z], zs_sem.at[v, d], zr_sem.at[v, plus_z(d)], {"row_0": z}
+            ).wait_recv()
+        )
+        total = mid[v, z]
         for d in range(1, nz):
-            own = own + into[plus_z(d)]
-        return own
-
-    def total_x(own, into):
-        for d in range(1, nx):
-            own = own + into[plus_x(d)]
-        return own
+            total = total + mid_in[v, plus_z(d)]
+        tile[v] = total
+
+    def sent_sum(v):
+        for d in whole:
+            whole_copy(v, d, x, plus_x(d)).wait_send()
+        for side in range(2):
+            hop_copy(v, side, 1).wait_send()
+            for hopped in range(2):
+                half_copy(v, side, hopped, hop.at[v, side], x, plus_x(1)).wait_send()
+        each_z(
+            lambda d: remote(mid.at[v, z], mid.at[v, z], zs_sem.at[v, d], zr_sem.at[v, z], {"row_0": z}).wait_send()
+        )
 
     def core_copy(src, dst, i):
         return remote(src, dst, cs_sem.at[i], cr_sem.at[i], {"col": other})
@@ -264,49 +324,33 @@
         def _():
             x_core.wait_recv()
 
-        prod[v] += dot(h_rows[1], rows[5 - 2 * v])
-
-        def blocks():
-            for j in range(2):
-                for q in range(2):
-                    block = prod[v, j * owners : (j + 1) * owners, q * LANES : (q + 1) * LANES]
-                    yield j * 2 + q, block.reshape(nx, nz, LANES)
-
-        @pl.when(v == 0)
-        def _():
-            for row, block in blocks():
-                y_part[:, :, row, :] = block
-            scatter_x(y_part, y_in, yxs_sem, yxr_sem)
+        value = prod[v] + dot(h_rows[1], rows[5 - 2 * v])
+        for j in range(2):
+            for q in range(2):
+                block = value[j * owners : (j + 1) * owners, q * LANES : (q + 1) * LANES]
+                part[v, :, :, j * 2 + q, :] = block.reshape(nx, nz, LANES)
 
         @pl.when(v == 1)
         def _():
-            for row, block in blocks():
-                for owner_x in range(nx):
-                    x_part[:, owner_x, row, :] = block[owner_x]
-            scatter_z(x_part, x_in, xzs_sem, xzr_sem)
+            hop_on(0)
+
+        start_sum(v)
 
     loop(0, 2, other_product)
-
-    got_all_x(y_in, yxs_sem, yxr_sem)
-    y_mid[...] = total_x(y_part[x], y_in)
-    scatter_z(y_mid, y_mid_in, yzs_sem, yzr_sem)
+    sum_x(0)
+    hop_on(1)
+    sum_x(1)
 
     got_all_z(nb_all_z, nzs_sem, nzr_sem)
     nb_all_z[z] = nb_tile[...]
     send_all_x(nb_all_z, gathered.at[0], nxs_sem, nxr_sem)
     gathered[0, x] = nb_all_z[...]
 
-    got_all_z(x_in, xzs_sem, xzr_sem)
-    x_mid[...] = total_z(x_part[z], x_in)
-    scatter_x(x_mid, x_mid_in, xxs_sem, xxr_sem)
-
-    got_all_z(y_mid_in, yzs_sem, yzr_sem)
-    tile[0] = total_z(y_mid[z], y_mid_in)
+    sum_z(0)
     send_all_z(tile.at[0], all_z, gzs_sem, gzr_sem)
     all_z[z] = tile[0]
 
-    got_all_x(x_mid_in, xxs_sem, xxr_sem)
-    tile[1] = total_x(x_mid[x], x_mid_in)
+    sum_z(1)
     for q in range(2):
         squares = 0.0
         for j in range(2):
@@ -396,10 +440,7 @@
             y_core.wait_send()
             x_core.wait_send()
             sent_all_z(nb_tile, nzs_sem, nzr_sem)
-            sent_all_x(y_part.at[x], yxs_sem, yxr_sem)
-            sent_all_z(y_mid.at[z], yzs_sem, yzr_sem)
-            sent_all_z(x_part.at[z], xzs_sem, xzr_sem)
-            sent_all_x(x_mid.at[x], xxs_sem, xxr_sem)
+            loop(0, 2, sent_sum)
             sent_all_x(nb_all_z, nxs_sem, nxr_sem)
             sent_all_z(tile.at[0], gzs_sem, gzr_sem)
 
@@ -465,9 +506,10 @@
     sems = pltpu.SemaphoreType.DMA
     sem_shapes = (
         [(8,)]
-        + [(nx,)] * 2
-        + [(nz,)] * 4
-        + [(nx,)] * 2
+        + [(2, nx)] * 2
+        + [(2, 2, 2)] * 2
+        + [(2, 2)] * 2
+        + [(2, nz)] * 2
         + [(nz,)] * 2
         + [(groups, nx)] * 2
         + [(nz,)] * 2
@@ -489,14 +531,12 @@
             buffer(6, *square),
             buffer(2, 2 * owners, block_width),
             buffer(2, 2 * owners, block_width),
-            buffer(nx, nz, *chunk),
-            buffer(nx, nz, *chunk),
-            buffer(nz, *chunk),
-            buffer(nz, *chunk),
-            buffer(nz, nx, *chunk),
-            buffer(nz, nx, *chunk),
-            buffer(nx, *chunk),
-            buffer(nx, *chunk),
+            buffer(2, nx, nz, *chunk),
+            buffer(2, nx, nz, *chunk),
+            buffer(2, 2, nz // 2, *chunk),
+            buffer(2, 2, nz // 2, *chunk),
+            buffer(2, nz, *chunk),
+            buffer(2, nz, *chunk),
             buffer(2, *chunk),
             buffer(nz, *chunk),
             buffer(2, nx, nz, *chunk),

time: 89.9 us -> 86.6 us (0.963)
  Pallas kernels: 89.2 us -> 85.8 us
    pallas_call x1, Pallas kernels: 88.3 us -> 84.9 us  [on_device(): pl.pallas_call(functools.partial(kernel, nz, nx), out_shape=(f32((8, bloc...]
where the time goes in v7:
time: 86.6 us; the launch traced here: 86.4 us
  Pallas kernels  85.8 us (99%)
    pallas_call x1, Pallas kernels, on_device(): pl.pallas_call(functools.partial(kernel, nz, nx), out_shape=(f32((8, bloc...  84.9 us

profile of v7, /device:TPU:65, one launch (start us, length us, event | category | flops | bytes accessed | tf_op | source)
XLA Modules:
  0.0 86.4 jit_solution(17597011685499240893)
XLA Ops:
  0.6 84.9 %lobpcg_step.1 = (f32[8,256]{1,0:T(8,128)S(1)}, f32[256,256]{1,0:T(8,128)S(1)}, f32[256,256]{1,0:T(8,128)S(1)}) custom-call(f32[1024,128]{1,0:T(8,128)} %bitcast.6, f32[256,256]{1,0:T(8,128)} %x_hbm.1, f32[256,256]{1,0:T(8,128)} %w_hbm.1, f32[256,256]{1,0:T(8,128)} %p_hbm.1, f32[768,256]{1,0:T(8,128)} %c_hbm.1, f32[1,256]{1,0:T(1,128)} %bitcast.7), custom_call_target="tpu_custom_call" | custom-call | tf_op jit(solution)/shard_map/lobpcg_step/pallas_call | solution.py:522
  85.6 0.8 finish.1

commit v8 on v7

--- a/solution.py
+++ b/solution.py
@@ -23,14 +23,16 @@
     return jnp.dot(left, right, preferred_element_type=jnp.float32, precision=HIGHEST)
 
 
-def tdot(left, right):
-    return lax.dot_general(
-        left,
-        right,
-        (((0,), (0,)), ((), ())),
-        preferred_element_type=jnp.float32,
-        precision=HIGHEST,
-    )
+def halves(value):
+    high = value.astype(jnp.bfloat16)
+    return high, (value - high.astype(jnp.float32)).astype(jnp.bfloat16)
+
+
+def dot3(left, right):
+    left_high, left_low = halves(left)
+    right_high, right_low = halves(right)
+    f32_dot = functools.partial(jnp.dot, preferred_element_type=jnp.float32)
+    return f32_dot(left_high, right_high) + (f32_dot(left_high, right_low) + f32_dot(left_low, right_high))
 
 
 def kernel(
@@ -243,6 +245,19 @@
     def core_copy(src, dst, i):
         return remote(src, dst, cs_sem.at[i], cr_sem.at[i], {"col": other})
 
+    barrier = pltpu.get_barrier_semaphore()
+    def signal(device):
+        pl.semaphore_signal(barrier, inc=1, device_id=device, device_id_type=MESH)
+
+    def both_cores(body):
+        loop(1, 2 * nx, lambda n: body(n // nx, lax.rem(n, nx)))
+
+    def core_of(which):
+        return core + which * (1 - 2 * core)
+
+    each_z(lambda d: signal({"row_0": plus_z(d)}))
+    both_cores(lambda which, d: signal({"row_1": plus_x(d), "col": core_of(which)}))
+
     loads = []
     for i, (src, dst) in enumerate(
         [
@@ -259,19 +274,6 @@
         loads.append(pltpu.make_async_copy(src, dst, in_sem.at[i]))
         loads[i].start()
 
-    barrier = pltpu.get_barrier_semaphore()
-    def signal(device):
-        pl.semaphore_signal(barrier, inc=1, device_id=device, device_id_type=MESH)
-
-    def both_cores(body):
-        loop(1, 2 * nx, lambda n: body(n // nx, lax.rem(n, nx)))
-
-    def core_of(which):
-        return core + which * (1 - 2 * core)
-
-    each_z(lambda d: signal({"row_0": plus_z(d)}))
-    both_cores(lambda which, d: signal({"row_1": plus_x(d), "col": core_of(which)}))
-
     for load in loads[:6]:
         load.wait()
 
@@ -279,7 +281,7 @@
 
     def add_product(i):
         small_ref[2:4, :] = rows[4, 0:2, :]
-        rows[4] += dot(rows[i], c_ref[i])
+        rows[4] += dot3(rows[i], c_ref[i])
 
     loop(0, 3, add_product)
     small_ref[0:2, :] = rows[4, 0:2, :]
@@ -304,10 +306,8 @@
 
     loop(0, 2 * nx, order)
 
-    def own_product(v):
-        prod[v] = dot(h_rows[0], rows[4 - 2 * v])
-
-    loop(0, 2, own_product)
+    prod[0] = dot3(h_rows[0], rows[4])
+    prod[1] = dot(h_rows[0], rows[2])
     pl.semaphore_wait(barrier, nz - 1 + 2 * nx - 1)
     y_core = core_copy(rows.at[4], rows.at[5], 1)
     y_core.start()
@@ -319,15 +319,16 @@
         @pl.when(v == 0)
         def _():
             y_core.wait_recv()
+            prod[0] += dot3(h_rows[1], rows[5])
 
         @pl.when(v == 1)
         def _():
             x_core.wait_recv()
-
-        value = prod[v] + dot(h_rows[1], rows[5 - 2 * v])
+            prod[1] += dot(h_rows[1], rows[3])
+
         for j in range(2):
             for q in range(2):
-                block = value[j * owners : (j + 1) * owners, q * LANES : (q + 1) * LANES]
+                block = prod[v, j * owners : (j + 1) * owners, q * LANES : (q + 1) * LANES]
                 part[v, :, :, j * 2 + q, :] = block.reshape(nx, nz, LANES)
 
         @pl.when(v == 1)
@@ -432,7 +433,7 @@
 
             loop(0, groups, got_group)
 
-        core_own[u] = dot(nb_t[...], rows_of(u))
+        core_own[u] = dot3(nb_t[...], rows_of(u))
         remote(core_own.at[u], core_par.at[u], cs_sem.at[2 + u], cr_sem.at[2 + u], {"col": other}).start()
 
         @pl.when(u == 0)

time: 86.6 us -> 87.3 us (level)
  no operation moved by 1% of the time
where the time goes in v8:
time: 87.3 us; the launch traced here: 87.1 us
  Pallas kernels  86.5 us (99%)
    pallas_call x1, Pallas kernels, on_device(): pl.pallas_call(functools.partial(kernel, nz, nx), out_shape=(f32((8, bloc...  85.7 us

profile of v8, /device:TPU:65, one launch (start us, length us, event | category | flops | bytes accessed | tf_op | source)
XLA Modules:
  0.0 87.1 jit_solution(14293226723006721522)
XLA Ops:
  0.6 85.7 %lobpcg_step.1 = (f32[8,256]{1,0:T(8,128)S(1)}, f32[256,256]{1,0:T(8,128)S(1)}, f32[256,256]{1,0:T(8,128)S(1)}) custom-call(f32[1024,128]{1,0:T(8,128)} %bitcast.6, f32[256,256]{1,0:T(8,128)} %x_hbm.1, f32[256,256]{1,0:T(8,128)} %w_hbm.1, f32[256,256]{1,0:T(8,128)} %p_hbm.1, f32[768,256]{1,0:T(8,128)} %c_hbm.1, f32[1,256]{1,0:T(1,128)} %bitcast.7), custom_call_target="tpu_custom_call" | custom-call | tf_op jit(solution)/shard_map/lobpcg_step/pallas_call | solution.py:523
  86.3 0.8 finish.1
